TPU v7x, 128 devices: a whole 4x4x4 slice. The times are simulated.
128 devices in a mesh: gx: 16 (over z, y), gy: 8 (over x, core).
Axes of the slice: x: 4, y: 4, z: 4, core: 2. Of those that a mesh axis runs over, the one named last changes fastest.
Arguments:
- spectra: bfloat16 [128, 256, 2048], P('gx', 'gy'), may hold values from -48 to 48
- resample_index: int32 [2048], replicated, may hold values from 0 to 2046
- resample_weight: float32 [2048], replicated, may hold values from 0 to 1
- disp_phase: float32 [2048], replicated, may hold values from -3.140625 to 3.140625
- surface_block: int32 [128, 256], P('gx', 'gy'), may hold values from 0 to 3
Outputs:
- enface: float32 [640, 128, 256], P(('gx', 'gy'))
All inputs are finite; a program needn't handle non-finite values.
Results may differ from a plain program's by a relative error of at most 0.003.
Values sent between devices are 32-bit elements; how exact they have to be, the bound alone decides.
A program may use at most 64 MiB of HBM per device.

v0:
```python
import math

import jax
import jax.numpy as jnp
from jax import lax
from jax.sharding import Mesh
from jax.sharding import PartitionSpec as P

BLOCK = 128
KEEP = 5
GX_GY = ("gx_0", "gx_1", "gy_0", "gy_1")
GX = ("gx_0", "gx_1")
GY = ("gy_0", "gy_1")


def by_axis(x, axes):
    for axis in axes:
        x = lax.psum(x, axis)
    return x


def dft_table(samples, block):
    depths = samples // 2
    blocks = depths // block
    rows = jnp.arange(samples, dtype=jnp.int32)
    cols = jnp.arange(depths, dtype=jnp.int32)
    turns = (rows[:, None] * cols[None, :] % samples).astype(jnp.float32)
    angle = 2.0 * math.pi / samples * turns
    cosine = jnp.cos(angle).astype(jnp.bfloat16).reshape(samples, blocks, block)
    sine = jnp.sin(angle).astype(jnp.bfloat16).reshape(samples, blocks, block)
    upper = jnp.concatenate([cosine, -sine], axis=2)
    lower = jnp.concatenate([sine, cosine], axis=2)
    return jnp.concatenate([upper, lower], axis=0)


def resample_matrix(samples, resample_index, resample_weight):
    source = jnp.arange(samples, dtype=jnp.int32)[:, None]
    left_hit = (source == resample_index[None, :]).astype(jnp.float32)
    right_hit = (source == resample_index[None, :] + 1).astype(jnp.float32)
    return left_hit * (1.0 - resample_weight)[None, :] + right_hit * resample_weight[None, :]


def phase_planes(lines, resample_index, resample_weight, disp_phase):
    matrix = resample_matrix(lines.shape[1], resample_index, resample_weight)
    resampled = jnp.dot(
        lines.astype(jnp.float32),
        matrix,
        precision=lax.Precision.HIGHEST,
        preferred_element_type=jnp.float32,
    )
    real_part = (resampled * jnp.cos(disp_phase)).astype(jnp.bfloat16)
    imag_part = (resampled * jnp.sin(disp_phase)).astype(jnp.bfloat16)
    return jnp.concatenate([real_part, imag_part], axis=1)


def select_blocks(power, surface):
    blocks = power.shape[1]
    wanted = surface[:, None] + jnp.arange(KEEP, dtype=jnp.int32)[None, :]
    chooser = wanted[:, :, None] == jnp.arange(blocks, dtype=jnp.int32)[None, None, :]
    chosen = jnp.where(chooser[:, :, :, None], power[:, None, :, :], 0.0)
    return jnp.sum(chosen, axis=2)


def on_device(spectra, resample_index, resample_weight, disp_phase, surface_block):
    across, along, samples = spectra.shape
    count = across * along
    blocks = samples // (2 * BLOCK)
    table = dft_table(samples, BLOCK)
    lines = spectra.reshape(count, samples)
    stacked = phase_planes(lines, resample_index, resample_weight, disp_phase)
    surface = surface_block.reshape(count)
    depth = jnp.dot(
        stacked, table.reshape(2 * samples, blocks * 2 * BLOCK), preferred_element_type=jnp.float32
    )
    depth = depth.reshape(count, blocks, 2, BLOCK)
    power = depth[:, :, 0] * depth[:, :, 0] + depth[:, :, 1] * depth[:, :, 1]
    kept = select_blocks(power, surface).reshape(count, KEEP * BLOCK)
    total = by_axis(jnp.sum(kept), GX_GY)
    width_x = lax.axis_size(GX)
    width_y = lax.axis_size(GY)
    level = total / (count * KEEP * BLOCK * width_x * width_y) + 1e-06
    image = jnp.log1p(kept / level)
    slabs = jnp.transpose(image.reshape(across, along, KEEP * BLOCK), (2, 0, 1))
    moved = lax.all_to_all(
        slabs.reshape(KEEP * BLOCK, 1, across, along),
        GX_GY,
        split_axis=0,
        concat_axis=1,
        tiled=True,
    )
    rows_out = moved.shape[0]
    moved = moved.reshape(rows_out, width_x, width_y, across, along)
    placed = jnp.transpose(moved, (0, 1, 3, 2, 4))
    return placed.reshape(rows_out, width_x * across, width_y * along)


def solution(mesh):
    torus = Mesh(mesh.devices.reshape(4, 4, 4, 2), ("gx_0", "gx_1", "gy_0", "gy_1"))
    placed = (P(GX, GY, None), P(), P(), P(), P(GX, GY))
    return jax.shard_map(
        on_device, mesh=torus, in_specs=placed, out_specs=P(GX_GY, None, None), check_vma=False
    )
```

profile of v0, /device:TPU:1, one launch (start us, length us, event | category | flops | bytes accessed | tf_op | source)
XLA Modules:
  0.0 178.2 jit_solution(15800995466608411539)
XLA Ops:
  0.0 34.5 %sine_convert_fusion = (bf16[2048,8,128]{0,2,1:T(8,128)(2,1)S(1)}, bf16[2048,8,128]{0,2,1:T(8,128)(2,1)S(1)}) fusion(s32[8,128]{1,0:T(8,128)S(1)} %multiply_add_fusion), kind=kLoop, calls=%fused_computation.13 | loop fusion | flops 33554432 | bytes 8392704 | tf_op jit(solution)/shard_map/convert_element_type | solution.py:30
  34.5 32.3 %fusion.18 = bf16[2048,8,128]{0,2,1:T(8,128)(2,1)S(1)} fusion(s32[8,128]{1,0:T(8,128)S(1)} %multiply_add_fusion), kind=kLoop, calls=%fused_computation.31 | loop fusion | flops 37748736 | bytes 4198400 | tf_op jit(solution)/shard_map/neg | solution.py:31
  66.9 6.9 %maximum_maximum_fusion = bf16[4096,8,256]{0,2,1:T(8,128)(2,1)} fusion(bf16[2048,8,128]{0,2,1:T(8,128)(2,1)S(1)} %get-tuple-element.12, bf16[2048,8,128]{0,2,1:T(8,128)(2,1)S(1)} %get-tuple-element.11, bf16[2048,8,128]{0,2,1:T(8,128)(2,1)S(1)} %fusion.18), kind=kLoop, calls=%fused_computation | loop fusion | flops 67108864 | bytes 29360128 | tf_op jit(solution)/shard_map/concatenate | solution.py:33
  73.8 16.2 %fusion.19 = (bf16[256,2048]{0,1:T(8,128)(2,1)S(1)}, bf16[256,2048]{0,1:T(8,128)(2,1)S(1)}) fusion(f32[2048]{0:T(1024)S(1)} %get-tuple-element.9, f32[2048]{0:T(1024)S(1)} %get-tuple-element.10, bf16[256,2048]{1,0:T(8,128)(2,1)S(1)} %bitcast.29, f32[2048]{0:T(1024)S(1)} %copy-done.2, s32[2048]{0:T(1024)S(1)} %broadcast_add_fusion, ...), kind=kOutput, calls=%fused_computation.32 | convolution fusion | flops 12907970560 | bytes 3194880 | tf_op jit(solution)/shard_map/dot_general | solution.py:45
  90.1 8.7 %fusion.15 = f32[256,8,2,128]{3,0,2,1:T(8,128)S(1)} fusion(bf16[8,2,128,4096]{3,2,1,0:T(8,128)(2,1)} %bitcast.30, bf16[256,2048]{0,1:T(8,128)(2,1)S(1)} %get-tuple-element.8, bf16[256,2048]{0,1:T(8,128)(2,1)S(1)} %get-tuple-element.7), kind=kOutput, calls=%fused_computation.26 | convolution fusion | flops 4299161600 | bytes 20971520 | tf_op jit(solution)/shard_map/dot_general | solution.py:72
  98.7 0.1 fusion.22
  98.8 0.6 copy.23
  99.6 0.1 iota_add_fusion
  99.7 0.3 iota_compare_fusion.4
  100.0 3.1 %select_reduce_fusion = (f32[]{:T(128)}, f32[256,5,128]{2,1,0:T(8,128)S(1)}) fusion(f32[256,8,128]{2,1,0:T(8,128)S(1)} %copy.23, pred[256,5,8]{2,1,0:T(8,128)(4,1)S(1)} %iota_compare_fusion.4), kind=kLoop, calls=%fused_computation.23 | loop fusion | flops 3768319 | bytes 1714180 | tf_op jit(solution)/shard_map/reduce_sum | solution.py:78
  103.1 11.2 %psum.28 = f32[]{:T(128)} all-reduce(f32[]{:T(128)} %get-tuple-element.5), channel_id=1, replica_groups=mesh['gx_0'=4,'gx_1'=4,'gy_0'=4,'gy_1'=2] {'gx_0'}, use_global_device_ids=true, to_apply=%region_2.3 | all-reduce | flops 1 | bytes 8 | tf_op jit(solution)/shard_map/psum | solution.py:18
  114.3 9.6 %psum.29 = f32[]{:T(128)} all-reduce(f32[]{:T(128)} %psum.28), channel_id=1, replica_groups=mesh['gx_0'=4,'gx_1'=4,'gy_0'=4,'gy_1'=2] {'gx_1'}, use_global_device_ids=true, to_apply=%region_3.4 | all-reduce | flops 1 | bytes 8 | tf_op jit(solution)/shard_map/psum | solution.py:18
  123.8 9.1 %psum.30 = f32[]{:T(128)} all-reduce(f32[]{:T(128)} %psum.29), channel_id=1, replica_groups=mesh['gx_0'=4,'gx_1'=4,'gy_0'=4,'gy_1'=2] {'gy_0'}, use_global_device_ids=true, to_apply=%region_4.5 | all-reduce | flops 1 | bytes 8 | tf_op jit(solution)/shard_map/psum | solution.py:18
  132.9 9.2 %psum.31 = f32[]{:T(128)} all-reduce(f32[]{:T(128)} %psum.30), channel_id=1, replica_groups=mesh['gx_0'=4,'gx_1'=4,'gy_0'=4,'gy_1'=2] {'gy_1'}, use_global_device_ids=true, to_apply=%region_5.6 | all-reduce | flops 1 | bytes 8 | tf_op jit(solution)/shard_map/psum | solution.py:18
  142.8 0.3 divide_log-plus-one_fusion
  143.1 0.2 log1p.8
  143.3 2.1 %copy.24 = f32[640,1,8,32]{3,2,1,0:T(8,128)} copy(f32[640,1,8,32]{0,3,2,1:T(8,128)S(1)} %bitcast.32) | data formatting | bytes 1310720 | tf_op jit(solution)/shard_map/reshape | solution.py:85
  145.4 2.7 %reshape.98 = f32[128,1,1280]{2,1,0:T(1,128)S(1)} reshape(f32[640,1,8,32]{3,2,1,0:T(8,128)} %copy.24) | data formatting | bytes 1310720
  148.2 18.3 %all_to_all.15 = f32[128,1,1280]{2,1,0:T(1,128)S(1)} all-to-all(f32[128,1,1280]{2,1,0:T(1,128)S(1)} %reshape.98), channel_id=1, replica_groups=mesh['gx_0'=4,'gx_1'=4,'gy_0'=4,'gy_1'=2] {'gx_0','gx_1','gy_0','gy_1'}, dimensions={0} | all-to-all | bytes 1310720 | tf_op jit(solution)/shard_map/all_to_all | solution.py:84
  166.4 0.5 broadcast.80
  166.9 2.2 %reduce.2 = f32[128,1280]{1,0:T(8,128)S(1)} reduce(f32[128,1,1280]{2,1,0:T(1,128)S(1)} %all_to_all.15, f32[]{:T(128)} %broadcast.80), dimensions={1}, to_apply=%all_to_all.11.reduce_sub_computation | reduce | bytes 1310724 | tf_op jit(solution)/shard_map/all_to_all | solution.py:84
  169.1 2.3 %reshape.99 = f32[640,1,8,32]{3,2,1,0:T(8,128)} reshape(f32[128,1280]{1,0:T(8,128)S(1)} %reduce.2) | data formatting | bytes 1310720
  171.4 3.9 %copy.26 = f32[5,16,8,8,32]{4,3,2,1,0:T(8,128)} copy(f32[5,16,8,8,32]{4,2,0,3,1:T(8,128)} %bitcast.31) | data formatting | bytes 1310720 | tf_op jit(solution)/shard_map/transpose | solution.py:93
  175.3 2.9 %reshape.96 = f32[5,128,256]{2,1,0:T(8,128)} reshape(f32[5,16,8,8,32]{4,3,2,1,0:T(8,128)} %copy.26) | data formatting | bytes 1310720 | tf_op jit(solution)/shard_map/reshape | solution.py:94
  (15 shorter events, 0.2 us)
Async XLA Ops:
  0.0 73.8 %copy-start = (bf16[8,32,2048]{2,1,0:T(8,128)(2,1)S(1)}, bf16[8,32,2048]{2,1,0:T(8,128)(2,1)}, u32[]{:S(2)}) copy-start(bf16[8,32,2048]{2,1,0:T(8,128)(2,1)} %param.5) | copy-start | bytes 3145732
  0.0 66.8 %copy-start.1 = (f32[2048]{0:T(1024)S(1)}, f32[2048]{0:T(1024)}, u32[]{:S(2)}) copy-start(f32[2048]{0:T(1024)} %param.8) | copy-start | bytes 24580
  0.0 66.8 %copy-start.3 = (s32[2048]{0:T(1024)S(1)}, s32[2048]{0:T(1024)}, u32[]{:S(2)}) copy-start(s32[2048]{0:T(1024)} %param.6) | copy-start | bytes 24580
  0.0 66.9 %copy-start.2 = (f32[2048]{0:T(1024)S(1)}, f32[2048]{0:T(1024)}, u32[]{:S(2)}) copy-start(f32[2048]{0:T(1024)} %param.7) | copy-start | bytes 24580
  90.0 9.4 %copy-start.4 = (s32[8,32]{1,0:T(8,128)S(1)}, s32[8,32]{1,0:T(8,128)}, u32[]{:S(2)}) copy-start(s32[8,32]{1,0:T(8,128)} %param.9) | copy-start | bytes 3076
where the time goes:
time: 179 us; the launch traced here: 178 us
  other arithmetic  79.9 us (45%)
  blocking collectives  57.3 us (32%)
  matrix products  24.9 us (14%)
  local copies, waits for them, and re-layouts  15.4 us (9%)
    psum x4, blocking collectives, by_axis(): x = lax.psum(x, axis)  39 us
    convert_element_type x1, other arithmetic, dft_table(): sine = jnp.sin(angle).astype(jnp.bfloat16).reshape(samples, blocks, block)  34.5 us
    neg x1, other arithmetic, dft_table(): upper = jnp.concatenate([cosine, -sine], axis=2)  32.3 us
    all_to_all x1, blocking collectives, on_device(): lax.all_to_all(slabs.reshape(KEEP * BLOCK, 1, across, along), GX_GY, spli...  18.3 us
    dot_general x1, matrix products, phase_planes(): jnp.dot(lines.astype(jnp.float32), matrix, precision=lax.Precision.HIGHES...  16.2 us
    dot_general x1, matrix products, on_device(): jnp.dot(stacked, table.reshape(2 * samples, blocks * 2 * BLOCK), preferre...  8.65 us
    concatenate x1, other arithmetic, dft_table(): return jnp.concatenate([upper, lower], axis=0)  6.93 us
    unnamed x12, local copies, waits for them, and re-layouts  5.01 us

commit v1 on v0

v1 whole, which is shorter than its diff:
```python
import functools
import math

import jax
import jax.numpy as jnp
import numpy as np
from jax import lax
from jax.experimental import pallas as pl
from jax.experimental.pallas import tpu as pltpu
from jax.sharding import PartitionSpec as P

NK = 2048
BLOCK = 128
KEEP = 5
RADIX = 16
GX = 16
GY = 8
DEV = GX * GY
TX = 8
TY = 32
LINES = TX * TY
ROWS = KEEP * BLOCK // DEV
COUNT = 128 * 256 * KEEP * BLOCK
MESH = pl.DeviceIdType.MESH


def base_table():
    n = np.arange(RADIX)[:, None, None]
    r = np.arange(BLOCK)[None, :, None]
    m = np.arange(NK // RADIX)[None, None, :]
    angle = 2.0 * math.pi * (((RADIX * m + n) * r) % NK) / NK
    c, s = np.cos(angle), np.sin(angle)
    top = np.concatenate([c, s], axis=2)
    low = np.concatenate([-s, c], axis=2)
    return np.concatenate([top, low], axis=1).astype(np.float32)


def rot(z, k, n):
    re, im = z
    k = k % n
    if k == 0:
        return re, im
    if 4 * k == n:
        return im, -re
    if 2 * k == n:
        return -re, -im
    if 4 * k == 3 * n:
        return -im, re
    if 8 * k == n:
        h = math.sqrt(0.5)
        return h * (re + im), h * (im - re)
    if 8 * k == 3 * n:
        h = math.sqrt(0.5)
        return h * (im - re), -h * (re + im)
    c, s = math.cos(2 * math.pi * k / n), math.sin(2 * math.pi * k / n)
    return c * re + s * im, c * im - s * re


def add(a, b):
    return a[0] + b[0], a[1] + b[1]


def sub(a, b):
    return a[0] - b[0], a[1] - b[1]


def fft(z):
    n = len(z)
    if n == 1:
        return z
    even, odd = fft(z[0::2]), fft(z[1::2])
    odd = [rot(odd[k], k, n) for k in range(n // 2)]
    return [add(even[k], odd[k]) for k in range(n // 2)] + [
        sub(even[k], odd[k]) for k in range(n // 2)
    ]


def half_fft(z):
    n = len(z)
    even, odd = fft(z[0::2]), fft(z[1::2])
    return [add(even[k], rot(odd[k], k, n)) for k in range(n // 2)]


def local_kernel(spectra, par, surface, table, msg, part, z, y):
    nt = (((1,), (1,)), ((), ()))
    lines = jnp.concatenate(
        [spectra[2 * p + q] for q in range(2) for p in range(4)], axis=0
    )
    shifted = jnp.concatenate([lines[:, 1:], lines[:, :1]], axis=1)
    both = jnp.concatenate([lines, shifted], axis=0)
    col = lax.broadcasted_iota(jnp.int32, (BLOCK, NK), 1).astype(jnp.float32)
    for n in range(RADIX):
        index = par[:, n : n + 1]
        weight = par[:, RADIX + n : RADIX + n + 1]
        cosp = par[:, 2 * RADIX + n : 2 * RADIX + n + 1]
        sinp = par[:, 3 * RADIX + n : 3 * RADIX + n + 1]
        hit = jnp.where(col == index, 1.0, 0.0).astype(jnp.bfloat16)
        pair = lax.dot_general(hit, both, nt, preferred_element_type=jnp.float32)
        value = (1.0 - weight) * pair[:, :LINES] + weight * pair[:, LINES:]
        z[n, :BLOCK, :] = (value * cosp).astype(jnp.bfloat16)
        z[n, BLOCK:, :] = (value * sinp).astype(jnp.bfloat16)
    for n in range(RADIX):
        y[n] = jnp.dot(table[n], z[n], preferred_element_type=jnp.float32)

    def group(g, acc):
        r0 = pl.multiple_of(g * 8, 8)
        for q in range(2):
            lane = pl.ds(q * 128, 128)
            pts = [
                (y[n, pl.ds(r0, 8), lane], y[n, pl.ds(BLOCK + r0, 8), lane])
                for n in range(RADIX)
            ]
            power = [re * re + im * im for re, im in half_fft(pts)]
            top = surface[q : q + 1, :]
            for k in range(KEEP):
                kept = power[k]
                for s in range(1, 4):
                    kept = jnp.where(top == s, power[k + s], kept)
                acc = acc + kept
                msg[pl.ds(k * BLOCK + r0, 8), q, :] = kept
        return acc

    acc = lax.fori_loop(0, BLOCK // 8, group, jnp.zeros((8, 128), jnp.float32))
    part[...] = jnp.sum(acc, axis=0, keepdims=True).reshape(1, 1, 128)


def exchange_kernel(msg, part, recv, sums, sem):
    gx, gy = lax.axis_index("gx"), lax.axis_index("gy")
    me = gx * GY + gy

    def peer(i):
        dz, dy, dx, dc = i // 32, (i // 8) % 4, (i // 2) % 4, i % 2
        pz, py = (gx // 4 + dz) % 4, (gx % 4 + dy) % 4
        px, pc = (gy // 2 + dx) % 4, (gy % 2 + dc) % 2
        return pz * 4 + py, px * 2 + pc

    barrier = pltpu.get_barrier_semaphore()

    def greet(i, _):
        pl.semaphore_signal(barrier, inc=1, device_id=peer(i), device_id_type=MESH)
        return 0

    lax.fori_loop(1, DEV, greet, 0)
    own = pltpu.make_async_copy(msg.at[pl.ds(ROWS * me, ROWS)], recv.at[me], sem.at[4])
    own.start()
    own_sum = pltpu.make_async_copy(part, sums.at[pl.ds(me, 1)], sem.at[5])
    own_sum.start()
    pl.semaphore_wait(barrier, DEV - 1)

    def send(i, _):
        px, py = peer(i)
        pltpu.make_async_remote_copy(
            src_ref=msg.at[pl.ds(ROWS * (px * GY + py), ROWS)],
            dst_ref=recv.at[me],
            send_sem=sem.at[0],
            recv_sem=sem.at[1],
            device_id=(px, py),
            device_id_type=MESH,
        ).start()
        pltpu.make_async_remote_copy(
            src_ref=part,
            dst_ref=sums.at[pl.ds(me, 1)],
            send_sem=sem.at[2],
            recv_sem=sem.at[3],
            device_id=(px, py),
            device_id_type=MESH,
        ).start()
        return 0

    lax.fori_loop(1, DEV, send, 0)
    most = recv.at[pl.ds(0, DEV - 1)]
    few = sums.at[pl.ds(0, DEV - 1)]
    pltpu.make_async_copy(most, most, sem.at[0]).wait()
    pltpu.make_async_copy(few, few, sem.at[2]).wait()
    own.wait()
    own_sum.wait()
    pltpu.make_async_copy(few, few, sem.at[3]).wait()
    pltpu.make_async_copy(most, most, sem.at[1]).wait()


def place_kernel(recv, sums, out):
    level = jnp.sum(sums[...]) / COUNT + 1e-6
    lane = lax.broadcasted_iota(jnp.int32, (8, 128), 1) // TY
    sub_ = lax.broadcasted_iota(jnp.int32, (8, 128), 0) // 2
    step = (sub_ - lane) % 4

    def body(gx, _):
        x0 = pl.multiple_of(gx * TX, TX)
        for r in range(ROWS):
            for h in range(2):
                v = recv[pl.ds(gx * GY + 4 * h, 4), r].reshape(8, 128)
                w = v
                for k in range(1, 4):
                    turned = pltpu.roll(pltpu.roll(v, 2 * k, 0), (128 - TY * k) % 128, 1)
                    w = jnp.where(step == k, turned, w)
                out[r, pl.ds(x0, TX), h * 128 : (h + 1) * 128] = jnp.log1p(w / level)
        return 0

    lax.fori_loop(0, GX, body, 0)


def on_device(spectra, resample_index, resample_weight, disp_phase, surface_block):
    f32 = jnp.float32
    vm = pl.BlockSpec(memory_space=pltpu.VMEM)
    table = jnp.asarray(base_table(), jnp.bfloat16)
    par = jnp.concatenate(
        [
            resample_index.astype(f32).reshape(BLOCK, RADIX),
            resample_weight.reshape(BLOCK, RADIX),
            jnp.cos(disp_phase).reshape(BLOCK, RADIX),
            jnp.sin(disp_phase).reshape(BLOCK, RADIX),
        ],
        axis=1,
    )
    surface = jnp.transpose(surface_block.reshape(4, 2, TY), (1, 0, 2)).reshape(2, 128)
    msg, part = pl.pallas_call(
        local_kernel,
        out_shape=(
            jax.ShapeDtypeStruct((KEEP * BLOCK, 2, 128), f32),
            jax.ShapeDtypeStruct((1, 1, 128), f32),
        ),
        in_specs=[vm] * 4,
        out_specs=[vm] * 2,
        scratch_shapes=[
            pltpu.VMEM((RADIX, 2 * BLOCK, LINES), jnp.bfloat16),
            pltpu.VMEM((RADIX, 2 * BLOCK, LINES), f32),
        ],
        compiler_params=pltpu.CompilerParams(vmem_limit_bytes=48 * 1024 * 1024),
        name="local",
    )(spectra, par, surface, table)
    recv, sums = pl.pallas_call(
        exchange_kernel,
        out_shape=(
            jax.ShapeDtypeStruct((DEV, ROWS, 2, 128), f32),
            jax.ShapeDtypeStruct((DEV, 1, 128), f32),
        ),
        in_specs=[vm] * 2,
        out_specs=[vm] * 2,
        scratch_shapes=[pltpu.SemaphoreType.DMA((6,))],
        compiler_params=pltpu.CompilerParams(collective_id=0, has_side_effects=True),
        name="exchange",
    )(msg, part)
    return pl.pallas_call(
        place_kernel,
        out_shape=jax.ShapeDtypeStruct((ROWS, GX * TX, GY * TY), f32),
        in_specs=[vm] * 2,
        out_specs=vm,
        name="place",
    )(recv, sums)


def solution(mesh):
    return jax.shard_map(
        on_device,
        mesh=mesh,
        in_specs=(P("gx", "gy", None), P(), P(), P(), P("gx", "gy")),
        out_specs=P(("gx", "gy"), None, None),
        check_vma=False,
    )
```

time: 179 us -> 52.2 us (0.29)
  other arithmetic: 79.9 us -> 0.82 us
  blocking collectives: 57.3 us -> 0 us
  Pallas kernels: 0 us -> 44.2 us
  matrix products: 24.9 us -> 0 us
  local copies, waits for them, and re-layouts: 15.4 us -> 6.73 us
    pallas_call x0 -> x3, Pallas kernels: none -> 44.2 us  [the longest x1 28.7 us: on_device(): pl.pallas_call(exchange_kernel, out_shape=(jax.ShapeDtypeStruct((DEV, ROW...]
    psum x4 -> x0, blocking collectives: 39 us -> none  [by_axis(): x = lax.psum(x, axis)]
    convert_element_type x1, other arithmetic: 34.5 us -> 0.7 us  [on_device(): resample_index.astype(f32).reshape(BLOCK, RADIX)]
    neg x1 -> x0, other arithmetic: 32.3 us -> none  [dft_table(): upper = jnp.concatenate([cosine, -sine], axis=2)]
    dot_general x2 -> x0, matrix products: 24.9 us -> none  [the longest x1 16.2 us: phase_planes(): jnp.dot(lines.astype(jnp.float32), matrix, precision=lax.Precision.HIGHES...]
    all_to_all x1 -> x0, blocking collectives: 18.3 us -> none  [on_device(): lax.all_to_all(slabs.reshape(KEEP * BLOCK, 1, across, along), GX_GY, spli...]
    concatenate x1, other arithmetic: 6.93 us -> 0.12 us  [on_device(): jnp.concatenate([resample_index.astype(f32).reshape(BLOCK, RADIX), resamp...]
    transpose x1 -> x0, local copies, waits for them, and re-layouts: 3.87 us -> none  [on_device(): placed = jnp.transpose(moved, (0, 1, 3, 2, 4))]
where the time goes in v1:
time: 52.2 us; the launch traced here: 51.9 us
  Pallas kernels  44.2 us (85%)
  local copies, waits for them, and re-layouts  6.73 us (13%)
  other arithmetic  0.82 us (2%)
    pallas_call x1, Pallas kernels, on_device(): pl.pallas_call(exchange_kernel, out_shape=(jax.ShapeDtypeStruct((DEV, ROW...  28.7 us
    pallas_call x1, Pallas kernels, on_device(): pl.pallas_call(local_kernel, out_shape=(jax.ShapeDtypeStruct((KEEP * BLOC...  11.6 us
    unnamed x8, local copies, waits for them, and re-layouts  4.22 us
    pallas_call x1, Pallas kernels, on_device(): pl.pallas_call(place_kernel, out_shape=jax.ShapeDtypeStruct((ROWS, GX * T...  4.01 us

profile of v1, /device:TPU:1, one launch (start us, length us, event | category | flops | bytes accessed | tf_op | source)
XLA Modules:
  0.0 51.9 jit_solution(10439846388327227731)
XLA Ops:
  0.0 0.7 %copy.10 = s32[4,2,32]{2,0,1:T(4,128)S(1)} copy(s32[4,2,32]{2,1,0:T(2,128)} %bitcast.5) | data formatting | bytes 2048 | tf_op jit(solution)/shard_map/reshape | solution.py:215
  0.7 0.1 reshape.23.surface
  0.8 0.7 %convert_element_type.3 = f32[2048]{0:T(1024)S(1)} convert(s32[2048]{0:T(1024)} %param.7) | non-fusion elementwise | flops 2048 | bytes 16384 | tf_op jit(solution)/shard_map/convert_element_type | solution.py:208
  1.5 0.7 %fusion = (f32[2048]{0:T(1024)S(1)}, f32[2048]{0:T(1024)S(1)}) fusion(f32[2048]{0:T(1024)} %param.9), kind=kLoop, calls=%fused_computation.2 | loop fusion | bytes 24576 | tf_op jit(solution)/shard_map/cos | solution.py:210
  2.2 0.1 reshape.20
  2.3 0.1 reshape.18
  2.4 0.1 reshape.21
  2.5 0.8 %reshape.19 = f32[128,16]{1,0:T(8,128)S(1)} reshape(f32[2048]{0:T(1024)} %param.8) | data formatting | bytes 16384 | tf_op jit(solution)/shard_map/reshape | solution.py:209
  3.3 0.1 pad_maximum_fusion.par
  3.4 0.0 copy-start
  3.4 1.6 %copy-done = bf16[16,256,256]{2,1,0:T(8,128)(2,1)S(1)} copy-done((bf16[16,256,256]{2,1,0:T(8,128)(2,1)S(1)}, bf16[16,256,256]{2,1,0:T(8,128)(2,1)}, u32[]{:S(2)}) %copy-start) | copy-done | bytes 2097176
  5.0 0.0 copy-start.1
  5.0 1.2 %copy-done.1 = bf16[8,32,2048]{2,1,0:T(8,128)(2,1)S(1)} copy-done((bf16[8,32,2048]{2,1,0:T(8,128)(2,1)S(1)}, bf16[8,32,2048]{2,1,0:T(8,128)(2,1)}, u32[]{:S(2)}) %copy-start.1) | copy-done | bytes 1048600
  6.2 11.6 %local.1 = (f32[640,2,128]{2,1,0:T(2,128)S(1)}, f32[1,1,128]{2,1,0:T(1,128)S(1)}) custom-call(bf16[8,32,2048]{2,1,0:T(8,128)(2,1)S(1)} %copy-done.1, f32[128,64]{1,0:T(8,128)S(1)} %pad_maximum_fusion.par, s32[2,128]{1,0:T(2,128)S(1)} %reshape.23.surface, bf16[16,256,256]{2,1,0:T(8,128)(2,1)S(1)} %copy-done), custom_call_target="tpu_custom_call" | custom-call | tf_op jit(solution)/shard_map/local/pallas_call | solution.py:216
  17.8 0.0 copy-start.2
  17.8 0.8 %copy-done.2 = f32[640,2,128]{2,1,0:T(2,128)} copy-done((f32[640,2,128]{2,1,0:T(2,128)}, f32[640,2,128]{2,1,0:T(2,128)S(1)}, u32[]{:S(2)}) %copy-start.2) | copy-done | bytes 655384
  18.6 0.0 copy-start.3
  18.6 0.6 %copy-done.3 = f32[1,1,128]{2,1,0:T(1,128)} copy-done((f32[1,1,128]{2,1,0:T(1,128)}, f32[1,1,128]{2,1,0:T(1,128)S(1)}, u32[]{:S(2)}) %copy-start.3) | copy-done | bytes 536
  19.2 28.7 %exchange.1 = (f32[128,5,2,128]{3,2,1,0:T(2,128)}, f32[128,1,128]{2,1,0:T(1,128)}) custom-call(f32[640,2,128]{2,1,0:T(2,128)} %copy-done.2, f32[1,1,128]{2,1,0:T(1,128)} %copy-done.3), custom_call_target="tpu_custom_call" | custom-call | tf_op jit(solution)/shard_map/exchange/pallas_call | solution.py:231
  47.9 4.0 %place.1 = f32[5,128,256]{2,1,0:T(8,128)} custom-call(f32[128,5,2,128]{3,2,1,0:T(2,128)} %get-tuple-element.11.recv, f32[128,1,128]{2,1,0:T(1,128)} %get-tuple-element.12.sums), custom_call_target="tpu_custom_call" | custom-call | tf_op jit(solution)/shard_map/place/pallas_call | solution.py:243
Async XLA Ops:
  3.4 1.6 %copy-start = (bf16[16,256,256]{2,1,0:T(8,128)(2,1)S(1)}, bf16[16,256,256]{2,1,0:T(8,128)(2,1)}, u32[]{:S(2)}) copy-start(bf16[16,256,256]{2,1,0:T(8,128)(2,1)} %constant.2.clone.table) | copy-start | bytes 6291460
  5.0 1.2 %copy-start.1 = (bf16[8,32,2048]{2,1,0:T(8,128)(2,1)S(1)}, bf16[8,32,2048]{2,1,0:T(8,128)(2,1)}, u32[]{:S(2)}) copy-start(bf16[8,32,2048]{2,1,0:T(8,128)(2,1)} %spectra.1) | copy-start | bytes 3145732
  17.8 0.8 %copy-start.2 = (f32[640,2,128]{2,1,0:T(2,128)}, f32[640,2,128]{2,1,0:T(2,128)S(1)}, u32[]{:S(2)}) copy-start(f32[640,2,128]{2,1,0:T(2,128)S(1)} %get-tuple-element.9.msg) | copy-start | bytes 1966084
  18.6 0.6 %copy-start.3 = (f32[1,1,128]{2,1,0:T(1,128)}, f32[1,1,128]{2,1,0:T(1,128)S(1)}, u32[]{:S(2)}) copy-start(f32[1,1,128]{2,1,0:T(1,128)S(1)} %get-tuple-element.10.part) | copy-start | bytes 1540

commit v2 on v1

v2 whole, which is shorter than its diff:
```python
import functools
import math

import jax
import jax.numpy as jnp
import numpy as np
from jax import lax
from jax.experimental import pallas as pl
from jax.experimental.pallas import tpu as pltpu
from jax.sharding import PartitionSpec as P

NK = 2048
BLOCK = 128
KEEP = 5
RADIX = 16
GX = 16
GY = 8
DEV = GX * GY
TX = 8
TY = 32
LINES = TX * TY
ROWS = KEEP * BLOCK // DEV
COUNT = 128 * 256 * KEEP * BLOCK
MESH = pl.DeviceIdType.MESH


def base_table():
    c = np.arange(RADIX)[:, None, None]
    b = np.arange(NK // (2 * RADIX))[None, :, None]
    m = np.arange(BLOCK)[None, None, :]
    angle = 2.0 * math.pi * ((m * (RADIX * b + c)) % NK) / NK
    cos, sin = np.cos(angle), np.sin(angle)
    top = np.concatenate([cos, sin], axis=2)
    low = np.concatenate([-sin, cos], axis=2)
    return np.concatenate([top, low], axis=1).astype(np.float32)


def rot(z, k, n):
    re, im = z
    k = k % n
    if k == 0:
        return re, im
    if 4 * k == n:
        return im, -re
    if 2 * k == n:
        return -re, -im
    if 4 * k == 3 * n:
        return -im, re
    if 8 * k == n:
        h = math.sqrt(0.5)
        return h * (re + im), h * (im - re)
    if 8 * k == 3 * n:
        h = math.sqrt(0.5)
        return h * (im - re), -h * (re + im)
    c, s = math.cos(2 * math.pi * k / n), math.sin(2 * math.pi * k / n)
    return c * re + s * im, c * im - s * re


def add(a, b):
    return a[0] + b[0], a[1] + b[1]


def sub(a, b):
    return a[0] - b[0], a[1] - b[1]


def fft(z):
    n = len(z)
    if n == 1:
        return z
    even, odd = fft(z[0::2]), fft(z[1::2])
    odd = [rot(odd[k], k, n) for k in range(n // 2)]
    return [add(even[k], odd[k]) for k in range(n // 2)] + [
        sub(even[k], odd[k]) for k in range(n // 2)
    ]


def peer(i, gx, gy):
    dz, dy, dx, dc = i // 32, (i // 8) % 4, (i // 2) % 4, i % 2
    pz, py = (gx // 4 + dz) % 4, (gx % 4 + dy) % 4
    px, pc = (gy // 2 + dx) % 4, (gy % 2 + dc) % 2
    return pz * 4 + py, px * 2 + pc


def main_kernel(
    spectra, index, weight, phase, surface, table, recv, sums,
    both, params, idx, surf, tab, x, y, msg, part, load, sem,
):
    gx, gy = lax.axis_index("gx"), lax.axis_index("gy")
    me = gx * GY + gy
    barrier = pltpu.get_barrier_semaphore()
    f32 = jnp.float32

    small = [
        pltpu.make_async_copy(index, idx, load.at[0]),
        pltpu.make_async_copy(weight, params.at[0], load.at[1]),
        pltpu.make_async_copy(phase, params.at[1], load.at[2]),
        pltpu.make_async_copy(surface, surf, load.at[3]),
    ]
    tiles = [
        pltpu.make_async_copy(
            spectra.at[2 * p + q], both.at[pl.ds((4 * q + p) * TY, TY)], load.at[4 + 4 * q + p]
        )
        for q in range(2)
        for p in range(4)
    ]
    big = pltpu.make_async_copy(table, tab, load.at[12])
    for copy in tiles + small + [big]:
        copy.start()

    def greet(i, _):
        pl.semaphore_signal(barrier, inc=1, device_id=peer(i, gx, gy), device_id_type=MESH)
        return 0

    lax.fori_loop(1, DEV, greet, 0)

    for copy in tiles + small:
        copy.wait()
    lines = both[:LINES, :]
    both[LINES:, :] = jnp.concatenate([lines[:, 1:], lines[:, :1]], axis=1)
    row = lax.broadcasted_iota(jnp.int32, (NK, 2 * BLOCK), 0)
    for j in range(RADIX // 2):
        pick = jnp.concatenate([idx[2 * j : 2 * j + 1, :], idx[2 * j + 1 : 2 * j + 2, :]], axis=1)
        hit = jnp.where(row == pick, 1.0, 0.0).astype(jnp.bfloat16)
        pair = jnp.dot(both[...], hit, preferred_element_type=f32)
        for h in range(2):
            lane = slice(h * BLOCK, (h + 1) * BLOCK)
            w = params[0, 2 * j + h : 2 * j + h + 1, :]
            x[2 * j + h] = (1.0 - w) * pair[:LINES, lane] + w * pair[LINES:, lane]
    cosp = jnp.cos(params[1])
    sinp = jnp.sin(params[1])
    params[0] = cosp
    params[1] = sinp

    def spread(g, _):
        r0 = pl.multiple_of(g * 16, 16)
        halves = []
        for h in range(2):
            value = [x[n, pl.ds(r0 + 8 * h, 8), :] for n in range(RADIX)]
            halves.append(
                fft([(v * params[0, n : n + 1, :], v * params[1, n : n + 1, :]) for n, v in enumerate(value)])
            )
        for c in range(RADIX):
            for o in range(2):
                both_rows = jnp.concatenate([halves[0][c][o], halves[1][c][o]], axis=0)
                y[c, pl.ds(r0, 16), o * BLOCK : (o + 1) * BLOCK] = both_rows.astype(jnp.bfloat16)
        return 0

    lax.fori_loop(0, LINES // 16, spread, 0)
    big.wait()
    nt = (((1,), (1,)), ((), ()))
    tops = [
        jnp.concatenate([surf[2 * p + q : 2 * p + q + 1, :] for p in range(4)], axis=1)
        for q in range(2)
    ]
    acc = jnp.zeros((8, 128), f32)
    for c in range(RADIX):
        depth = lax.dot_general(tab[c], y[c], nt, preferred_element_type=f32)
        power = depth[:64] * depth[:64] + depth[64:] * depth[64:]
        for q in range(2):
            tile = [power[8 * b : 8 * b + 8, q * 128 : (q + 1) * 128] for b in range(8)]
            for k in range(KEEP):
                kept = tile[k]
                for s in range(1, 4):
                    kept = jnp.where(tops[q] == s, tile[k + s], kept)
                acc = acc + kept
                msg[pl.ds(k * BLOCK + c, 8, stride=RADIX), q, :] = kept
    part[...] = jnp.sum(acc, axis=0, keepdims=True).reshape(1, 1, 128)

    own = pltpu.make_async_copy(msg.at[pl.ds(ROWS * me, ROWS)], recv.at[me], sem.at[4])
    own.start()
    own_sum = pltpu.make_async_copy(part, sums.at[pl.ds(me, 1)], sem.at[5])
    own_sum.start()
    pl.semaphore_wait(barrier, DEV - 1)

    def send(i, _):
        px, py = peer(DEV - i, gx, gy)
        pltpu.make_async_remote_copy(
            src_ref=part,
            dst_ref=sums.at[pl.ds(me, 1)],
            send_sem=sem.at[2],
            recv_sem=sem.at[3],
            device_id=(px, py),
            device_id_type=MESH,
        ).start()
        pltpu.make_async_remote_copy(
            src_ref=msg.at[pl.ds(ROWS * (px * GY + py), ROWS)],
            dst_ref=recv.at[me],
            send_sem=sem.at[0],
            recv_sem=sem.at[1],
            device_id=(px, py),
            device_id_type=MESH,
        ).start()
        return 0

    lax.fori_loop(1, DEV, send, 0)
    most = recv.at[pl.ds(0, DEV - 1)]
    few = sums.at[pl.ds(0, DEV - 1)]
    pltpu.make_async_copy(most, most, sem.at[0]).wait()
    pltpu.make_async_copy(few, few, sem.at[2]).wait()
    own.wait()
    own_sum.wait()
    pltpu.make_async_copy(few, few, sem.at[3]).wait()
    pltpu.make_async_copy(most, most, sem.at[1]).wait()


def place_kernel(recv, sums, out):
    level = jnp.sum(sums[...]) / COUNT + 1e-6
    lane = lax.broadcasted_iota(jnp.int32, (8, 128), 1) // TY
    sub_ = lax.broadcasted_iota(jnp.int32, (8, 128), 0) // 2
    step = (sub_ - lane) % 4

    def body(gx, _):
        x0 = pl.multiple_of(gx * TX, TX)
        for r in range(ROWS):
            for h in range(2):
                v = recv[pl.ds(gx * GY + 4 * h, 4), r].reshape(8, 128)
                w = v
                for k in range(1, 4):
                    turned = pltpu.roll(pltpu.roll(v, 2 * k, 0), (128 - TY * k) % 128, 1)
                    w = jnp.where(step == k, turned, w)
                out[r, pl.ds(x0, TX), h * 128 : (h + 1) * 128] = jnp.log1p(w / level)
        return 0

    lax.fori_loop(0, GX, body, 0)


def on_device(spectra, resample_index, resample_weight, disp_phase, surface_block):
    f32 = jnp.float32
    bf16 = jnp.bfloat16
    vm = pl.BlockSpec(memory_space=pltpu.VMEM)
    hbm = pl.BlockSpec(memory_space=pltpu.HBM)
    table = jnp.asarray(base_table(), bf16)
    recv, sums = pl.pallas_call(
        main_kernel,
        out_shape=(
            jax.ShapeDtypeStruct((DEV, ROWS, 2, 128), f32),
            jax.ShapeDtypeStruct((DEV, 1, 128), f32),
        ),
        in_specs=[hbm] * 6,
        out_specs=[vm] * 2,
        scratch_shapes=[
            pltpu.VMEM((2 * LINES, NK), bf16),
            pltpu.VMEM((2, RADIX, BLOCK), f32),
            pltpu.VMEM((RADIX, BLOCK), jnp.int32),
            pltpu.VMEM((TX, TY), jnp.int32),
            pltpu.VMEM((RADIX, BLOCK, 2 * BLOCK), bf16),
            pltpu.VMEM((RADIX, LINES, BLOCK), f32),
            pltpu.VMEM((RADIX, LINES, 2 * BLOCK), bf16),
            pltpu.VMEM((KEEP * BLOCK, 2, 128), f32),
            pltpu.VMEM((1, 1, 128), f32),
            pltpu.SemaphoreType.DMA((13,)),
            pltpu.SemaphoreType.DMA((6,)),
        ],
        compiler_params=pltpu.CompilerParams(
            collective_id=0, has_side_effects=True, vmem_limit_bytes=48 * 1024 * 1024
        ),
        name="main",
    )(
        spectra,
        resample_index.reshape(RADIX, BLOCK),
        resample_weight.reshape(RADIX, BLOCK),
        disp_phase.reshape(RADIX, BLOCK),
        surface_block,
        table,
    )
    return pl.pallas_call(
        place_kernel,
        out_shape=jax.ShapeDtypeStruct((ROWS, GX * TX, GY * TY), f32),
        in_specs=[vm] * 2,
        out_specs=vm,
        name="place",
    )(recv, sums)


def solution(mesh):
    return jax.shard_map(
        on_device,
        mesh=mesh,
        in_specs=(P("gx", "gy", None), P(), P(), P(), P("gx", "gy")),
        out_specs=P(("gx", "gy"), None, None),
        check_vma=False,
    )
```

time: 52.2 us -> 42 us (0.80)
  Pallas kernels: 44.2 us -> 35 us
  other arithmetic: 0.82 us -> 0 us
    pallas_call x2 -> x1, Pallas kernels: 40.2 us -> 31 us  [on_device(): pl.pallas_call(main_kernel, out_shape=(jax.ShapeDtypeStruct((DEV, ROWS, 2...]
    unnamed x8 -> x16, local copies, waits for them, and re-layouts: 4.22 us -> 6.68 us
    reshape x6 -> x0, local copies, waits for them, and re-layouts: 1.78 us -> none  [the longest x1 0.78 us: on_device(): resample_weight.reshape(BLOCK, RADIX)]
    cos x1 -> x0, local copies, waits for them, and re-layouts: 0.74 us -> none  [on_device(): jnp.cos(disp_phase).reshape(BLOCK, RADIX)]
    convert_element_type x1 -> x0, other arithmetic: 0.7 us -> none  [on_device(): resample_index.astype(f32).reshape(BLOCK, RADIX)]
where the time goes in v2:
time: 42 us; the launch traced here: 41.7 us
  Pallas kernels  35 us (83%)
  local copies, waits for them, and re-layouts  6.68 us (16%)
    pallas_call x1, Pallas kernels, on_device(): pl.pallas_call(main_kernel, out_shape=(jax.ShapeDtypeStruct((DEV, ROWS, 2...  31 us
    unnamed x16, local copies, waits for them, and re-layouts  6.68 us
    pallas_call x1, Pallas kernels, on_device(): pl.pallas_call(place_kernel, out_shape=jax.ShapeDtypeStruct((ROWS, GX * T...  4.01 us

profile of v2, /device:TPU:1, one launch (start us, length us, event | category | flops | bytes accessed | tf_op | source)
XLA Modules:
  0.0 41.7 jit_solution(7513182617633297938)
XLA Ops:
  0.0 0.0 copy-start.7
  0.0 0.7 %copy-done.7 = s32[8,32]{1,0:T(8,128)S(1)} copy-done((s32[8,32]{1,0:T(8,128)S(1)}, s32[8,32]{1,0:T(8,128)}, u32[]{:S(2)}) %copy-start.7) | copy-done | bytes 1048
  0.7 0.0 copy-start
  0.7 1.2 %copy-done = bf16[8,32,2048]{2,1,0:T(8,128)(2,1)S(1)} copy-done((bf16[8,32,2048]{2,1,0:T(8,128)(2,1)S(1)}, bf16[8,32,2048]{2,1,0:T(8,128)(2,1)}, u32[]{:S(2)}) %copy-start) | copy-done | bytes 1048600
  1.9 0.0 copy-start.1
  1.9 1.2 %copy-done.1 = bf16[16,128,256]{2,1,0:T(8,128)(2,1)S(1)} copy-done((bf16[16,128,256]{2,1,0:T(8,128)(2,1)S(1)}, bf16[16,128,256]{2,1,0:T(8,128)(2,1)}, u32[]{:S(2)}) %copy-start.1) | copy-done | bytes 1048600
  3.1 0.0 copy-start.4
  3.1 0.7 %copy-done.4 = s32[2048]{0:T(1024)S(1)} copy-done((s32[2048]{0:T(1024)S(1)}, s32[2048]{0:T(1024)}, u32[]{:S(2)}) %copy-start.4) | copy-done | bytes 8216
  3.8 0.0 copy-start.5
  3.8 0.7 %copy-done.5 = f32[2048]{0:T(1024)S(1)} copy-done((f32[2048]{0:T(1024)S(1)}, f32[2048]{0:T(1024)}, u32[]{:S(2)}) %copy-start.5) | copy-done | bytes 8216
  4.5 0.0 copy-start.6
  4.5 0.7 %copy-done.6 = f32[2048]{0:T(1024)S(1)} copy-done((f32[2048]{0:T(1024)S(1)}, f32[2048]{0:T(1024)}, u32[]{:S(2)}) %copy-start.6) | copy-done | bytes 8216
  5.2 31.0 %main.1 = (f32[128,5,2,128]{3,2,1,0:T(2,128)S(1)}, f32[128,1,128]{2,1,0:T(1,128)S(1)}) custom-call(bf16[8,32,2048]{2,1,0:T(8,128)(2,1)S(1)} %copy-done, s32[16,128]{1,0:T(8,128)S(1)} %bitcast.3, f32[16,128]{1,0:T(8,128)S(1)} %bitcast.4, f32[16,128]{1,0:T(8,128)S(1)} %bitcast.5, s32[8,32]{1,0:T(8,128)S(1)} %copy-done.7, bf16[16,128,256]{2,1,0:T(8,128)(2,1)S(1)} %copy-done.1), custom_call_target="tpu_custom_call" | custom-call | tf_op jit(solution)/shard_map/main/pallas_call | solution.py:234
  36.2 0.0 copy-start.2
  36.2 0.8 %copy-done.2 = f32[128,5,2,128]{3,2,1,0:T(2,128)} copy-done((f32[128,5,2,128]{3,2,1,0:T(2,128)}, f32[128,5,2,128]{3,2,1,0:T(2,128)S(1)}, u32[]{:S(2)}) %copy-start.2) | copy-done | bytes 655384
  37.0 0.0 copy-start.3
  37.1 0.6 %copy-done.3 = f32[128,1,128]{2,1,0:T(1,128)} copy-done((f32[128,1,128]{2,1,0:T(1,128)}, f32[128,1,128]{2,1,0:T(1,128)S(1)}, u32[]{:S(2)}) %copy-start.3) | copy-done | bytes 65560
  37.7 4.0 %place.1 = f32[5,128,256]{2,1,0:T(8,128)} custom-call(f32[128,5,2,128]{3,2,1,0:T(2,128)} %copy-done.2, f32[128,1,128]{2,1,0:T(1,128)} %copy-done.3), custom_call_target="tpu_custom_call" | custom-call | tf_op jit(solution)/shard_map/place/pallas_call | solution.py:267
Async XLA Ops:
  0.0 0.7 %copy-start.7 = (s32[8,32]{1,0:T(8,128)S(1)}, s32[8,32]{1,0:T(8,128)}, u32[]{:S(2)}) copy-start(s32[8,32]{1,0:T(8,128)} %surface.1) | copy-start | bytes 3076
  0.7 1.2 %copy-start = (bf16[8,32,2048]{2,1,0:T(8,128)(2,1)S(1)}, bf16[8,32,2048]{2,1,0:T(8,128)(2,1)}, u32[]{:S(2)}) copy-start(bf16[8,32,2048]{2,1,0:T(8,128)(2,1)} %spectra.1) | copy-start | bytes 3145732
  1.9 1.2 %copy-start.1 = (bf16[16,128,256]{2,1,0:T(8,128)(2,1)S(1)}, bf16[16,128,256]{2,1,0:T(8,128)(2,1)}, u32[]{:S(2)}) copy-start(bf16[16,128,256]{2,1,0:T(8,128)(2,1)} %constant.2.clone.table) | copy-start | bytes 3145732
  3.1 0.7 %copy-start.4 = (s32[2048]{0:T(1024)S(1)}, s32[2048]{0:T(1024)}, u32[]{:S(2)}) copy-start(s32[2048]{0:T(1024)} %param.7) | copy-start | bytes 24580
  3.8 0.7 %copy-start.5 = (f32[2048]{0:T(1024)S(1)}, f32[2048]{0:T(1024)}, u32[]{:S(2)}) copy-start(f32[2048]{0:T(1024)} %param.8) | copy-start | bytes 24580
  4.5 0.7 %copy-start.6 = (f32[2048]{0:T(1024)S(1)}, f32[2048]{0:T(1024)}, u32[]{:S(2)}) copy-start(f32[2048]{0:T(1024)} %param.9) | copy-start | bytes 24580
  36.2 0.8 %copy-start.2 = (f32[128,5,2,128]{3,2,1,0:T(2,128)}, f32[128,5,2,128]{3,2,1,0:T(2,128)S(1)}, u32[]{:S(2)}) copy-start(f32[128,5,2,128]{3,2,1,0:T(2,128)S(1)} %get-tuple-element.7.recv) | copy-start | bytes 1966084
  37.0 0.6 %copy-start.3 = (f32[128,1,128]{2,1,0:T(1,128)}, f32[128,1,128]{2,1,0:T(1,128)S(1)}, u32[]{:S(2)}) copy-start(f32[128,1,128]{2,1,0:T(1,128)S(1)} %get-tuple-element.8.sums) | copy-start | bytes 196612

commit v3 on v2

v3 whole, which is shorter than its diff:
```python
import itertools
import math

import jax
import jax.numpy as jnp
import numpy as np
from jax import lax
from jax.experimental import pallas as pl
from jax.experimental.pallas import tpu as pltpu
from jax.sharding import PartitionSpec as P

NK = 2048
BLOCK = 128
KEEP = 5
RADIX = 16
GX = 16
GY = 8
DEV = GX * GY
TX = 8
TY = 32
LINES = TX * TY
ROWS = KEEP * BLOCK // DEV
COUNT = 128 * 256 * KEEP * BLOCK
MESH = pl.DeviceIdType.MESH
VMEM_BYTES = 67043328


def base_table():
    c = np.arange(RADIX)[:, None, None]
    b = np.arange(NK // (2 * RADIX))[None, :, None]
    m = np.arange(BLOCK)[None, None, :]
    angle = 2.0 * math.pi * ((m * (RADIX * b + c)) % NK) / NK
    cos, sin = np.cos(angle), np.sin(angle)
    top = np.concatenate([cos, sin], axis=2)
    low = np.concatenate([-sin, cos], axis=2)
    return np.concatenate([top, low], axis=1).astype(np.float32)


def rot(z, k, n):
    re, im = z
    k = k % n
    if k == 0:
        return re, im
    if 4 * k == n:
        return im, -re
    if 2 * k == n:
        return -re, -im
    if 4 * k == 3 * n:
        return -im, re
    if 8 * k == n:
        h = math.sqrt(0.5)
        return h * (re + im), h * (im - re)
    if 8 * k == 3 * n:
        h = math.sqrt(0.5)
        return h * (im - re), -h * (re + im)
    c, s = math.cos(2 * math.pi * k / n), math.sin(2 * math.pi * k / n)
    return c * re + s * im, c * im - s * re


def add(a, b):
    return a[0] + b[0], a[1] + b[1]


def sub(a, b):
    return a[0] - b[0], a[1] - b[1]


def fft(z):
    n = len(z)
    if n == 1:
        return z
    even, odd = fft(z[0::2]), fft(z[1::2])
    odd = [rot(odd[k], k, n) for k in range(n // 2)]
    return [add(even[k], odd[k]) for k in range(n // 2)] + [
        sub(even[k], odd[k]) for k in range(n // 2)
    ]


def hops(o):
    return sum((0, 1, 2, 1)[v] for v in o[:3])


OFFSETS = sorted(
    [o for o in itertools.product(range(4), range(4), range(4), range(2)) if any(o)],
    key=lambda o: (-hops(o), o),
)


def main_kernel(
    spectra, index, weight, phase, surface, table, recv, sums,
    both, params, idx, surf, tab, hits, x, y, msg, part, load, sem,
):
    f32, bf16 = jnp.float32, jnp.bfloat16
    half = LINES // 2
    gx, gy = lax.axis_index("gx"), lax.axis_index("gy")
    me = gx * GY + gy
    zs = [(gx // 4 + d) % 4 for d in range(4)]
    ys = [(gx % 4 + d) % 4 for d in range(4)]
    xs = [(gy // 2 + d) % 4 for d in range(4)]
    cs = [(gy % 2 + d) % 2 for d in range(2)]
    zy = [[z * 4 + v for v in ys] for z in zs]
    xc = [[v * 2 + c for c in cs] for v in xs]
    peers = [(zy[o[0]][o[1]], xc[o[2]][o[3]]) for o in OFFSETS]
    barrier = pltpu.get_barrier_semaphore()

    small = [
        pltpu.make_async_copy(index, idx, load.at[0]),
        pltpu.make_async_copy(weight, params.at[0], load.at[1]),
        pltpu.make_async_copy(phase, params.at[1], load.at[2]),
        pltpu.make_async_copy(surface, surf, load.at[3]),
    ]
    tiles = [
        pltpu.make_async_copy(
            spectra.at[2 * p + q], both.at[q, pl.ds(p * TY, TY)], load.at[4 + 4 * q + p]
        )
        for q in range(2)
        for p in range(4)
    ]
    big = pltpu.make_async_copy(table, tab, load.at[12])
    for copy in small + tiles + [big]:
        copy.start()
    for to in peers:
        pl.semaphore_signal(barrier, inc=1, device_id=to, device_id_type=MESH)
    for copy in small:
        copy.wait()
    cosp = jnp.cos(params[1])
    sinp = jnp.sin(params[1])
    params[1] = cosp
    params[2] = sinp
    tops = [
        jnp.concatenate([surf[2 * p + q : 2 * p + q + 1, :] for p in range(4)], axis=1)
        for q in range(2)
    ]
    row = lax.broadcasted_iota(jnp.int32, (NK, 2 * BLOCK), 0)
    nt = (((1,), (1,)), ((), ()))

    def compute(q, acc):
        for copy in tiles[4 * q : 4 * q + 4]:
            copy.wait()
        lines = both[q, :half, :]
        both[q, half:, :] = jnp.concatenate([lines[:, 1:], lines[:, :1]], axis=1)
        for j in range(RADIX // 2):
            if q == 0:
                pick = jnp.concatenate(
                    [idx[2 * j : 2 * j + 1, :], idx[2 * j + 1 : 2 * j + 2, :]], axis=1
                )
                hits[j] = jnp.where(row == pick, 1.0, 0.0).astype(bf16)
            pair = jnp.dot(both[q], hits[j], preferred_element_type=f32)
            for h in range(2):
                lane = slice(h * BLOCK, (h + 1) * BLOCK)
                w = params[0, 2 * j + h : 2 * j + h + 1, :]
                x[2 * j + h] = (1.0 - w) * pair[:half, lane] + w * pair[half:, lane]

        def spread(g, _):
            r0 = pl.multiple_of(g * 16, 16)
            parts = []
            for n in range(RADIX):
                v = x[n, pl.ds(r0, 16), :]
                parts.append(
                    [
                        (v * params[1 + o, n : n + 1, :]).astype(bf16).astype(f32)
                        for o in range(2)
                    ]
                )
            low = fft([(re[:8], im[:8]) for re, im in parts])
            high = fft([(re[8:], im[8:]) for re, im in parts])
            for c in range(RADIX):
                for o in range(2):
                    rows = jnp.concatenate([low[c][o], high[c][o]], axis=0)
                    y[c, pl.ds(r0, 16), o * BLOCK : (o + 1) * BLOCK] = rows.astype(bf16)
            return 0

        lax.fori_loop(0, half // 16, spread, 0)
        if q == 0:
            big.wait()
        for c in range(RADIX):
            depth = lax.dot_general(tab[c], y[c], nt, preferred_element_type=f32)
            power = depth[:64] * depth[:64] + depth[64:] * depth[64:]
            tile = [power[8 * b : 8 * b + 8] for b in range(8)]
            for k in range(KEEP):
                kept = tile[k]
                for s in range(1, 4):
                    kept = jnp.where(tops[q] == s, tile[k + s], kept)
                acc = acc + kept
                msg[pl.ds((q * KEEP + k) * BLOCK + c, 8, stride=RADIX), 0, :] = kept
        return acc

    def slab(q, dest):
        return msg.at[pl.ds(q * KEEP * BLOCK + ROWS * dest, ROWS)]

    def landing(q):
        return recv.at[pl.ds((2 * me + q) * ROWS, ROWS)]

    def send(q):
        for px, py in peers:
            pltpu.make_async_remote_copy(
                src_ref=slab(q, px * GY + py),
                dst_ref=landing(q),
                send_sem=sem.at[2 * q],
                recv_sem=sem.at[2 * q + 1],
                device_id=(px, py),
                device_id_type=MESH,
            ).start()

    acc = compute(0, jnp.zeros((8, 128), f32))
    pl.semaphore_wait(barrier, DEV - 1)
    send(0)
    acc = compute(1, acc)
    part[...] = jnp.sum(acc, axis=0, keepdims=True).reshape(1, 1, 128)
    for px, py in peers:
        pltpu.make_async_remote_copy(
            src_ref=part,
            dst_ref=sums.at[pl.ds(me, 1)],
            send_sem=sem.at[4],
            recv_sem=sem.at[5],
            device_id=(px, py),
            device_id_type=MESH,
        ).start()
    send(1)
    own = [pltpu.make_async_copy(slab(q, me), landing(q), sem.at[6 + q]) for q in range(2)]
    own.append(pltpu.make_async_copy(part, sums.at[pl.ds(me, 1)], sem.at[8]))
    for copy in own:
        copy.start()
    for copy in own:
        copy.wait()
    most = recv.at[pl.ds(0, (DEV - 1) * ROWS)]
    few = sums.at[pl.ds(0, DEV - 1)]
    for ref, s in ((most, 0), (most, 2), (few, 4), (most, 1), (few, 5), (most, 3)):
        pltpu.make_async_copy(ref, ref, sem.at[s]).wait()


def place_kernel(recv, sums, out):
    level = jnp.sum(sums[...]) / COUNT + 1e-6
    scale = 1.0 / jnp.full((8, 128), level, jnp.float32)
    lane = lax.broadcasted_iota(jnp.int32, (8, 128), 1) // TY
    line = lax.broadcasted_iota(jnp.int32, (8, 128), 0) // 2
    step = (line - lane) % 4

    def body(gx, _):
        x0 = pl.multiple_of(gx * TX, TX)
        for h in range(2):
            for r in range(ROWS):
                v = recv[pl.ds((gx * GY + 4 * h) * 2 * ROWS + r, 8, stride=ROWS), 0, :]
                w = v
                for k in range(1, 4):
                    turned = pltpu.roll(pltpu.roll(v, 2 * k, 0), 128 - TY * k, 1)
                    w = jnp.where(step == k, turned, w)
                out[r, pl.ds(x0, TX), h * 128 : (h + 1) * 128] = jnp.log(1.0 + w * scale)
        return 0

    lax.fori_loop(0, GX, body, 0, unroll=2)


def on_device(spectra, resample_index, resample_weight, disp_phase, surface_block):
    f32 = jnp.float32
    bf16 = jnp.bfloat16
    vm = pl.BlockSpec(memory_space=pltpu.VMEM)
    hbm = pl.BlockSpec(memory_space=pltpu.HBM)
    table = jnp.asarray(base_table(), bf16)
    recv, sums = pl.pallas_call(
        main_kernel,
        out_shape=(
            jax.ShapeDtypeStruct((DEV * ROWS * 2, 1, 128), f32),
            jax.ShapeDtypeStruct((DEV, 1, 128), f32),
        ),
        in_specs=[hbm] * 6,
        out_specs=[vm] * 2,
        scratch_shapes=[
            pltpu.VMEM((2, LINES, NK), bf16),
            pltpu.VMEM((3, RADIX, BLOCK), f32),
            pltpu.VMEM((RADIX, BLOCK), jnp.int32),
            pltpu.VMEM((TX, TY), jnp.int32),
            pltpu.VMEM((RADIX, BLOCK, 2 * BLOCK), bf16),
            pltpu.VMEM((RADIX // 2, NK, 2 * BLOCK), bf16),
            pltpu.VMEM((RADIX, LINES // 2, BLOCK), f32),
            pltpu.VMEM((RADIX, LINES // 2, 2 * BLOCK), bf16),
            pltpu.VMEM((2 * KEEP * BLOCK, 1, 128), f32),
            pltpu.VMEM((1, 1, 128), f32),
            pltpu.SemaphoreType.DMA((13,)),
            pltpu.SemaphoreType.DMA((9,)),
        ],
        compiler_params=pltpu.CompilerParams(
            collective_id=0, has_side_effects=True, vmem_limit_bytes=VMEM_BYTES
        ),
        name="main",
    )(
        spectra,
        resample_index.reshape(RADIX, BLOCK),
        resample_weight.reshape(RADIX, BLOCK),
        disp_phase.reshape(RADIX, BLOCK),
        surface_block,
        table,
    )
    return pl.pallas_call(
        place_kernel,
        out_shape=jax.ShapeDtypeStruct((ROWS, GX * TX, GY * TY), f32),
        in_specs=[vm] * 2,
        out_specs=vm,
        name="place",
    )(recv, sums)


def solution(mesh):
    return jax.shard_map(
        on_device,
        mesh=mesh,
        in_specs=(P("gx", "gy", None), P(), P(), P(), P("gx", "gy")),
        out_specs=P(("gx", "gy"), None, None),
        check_vma=False,
    )
```

time: 42 us -> 29.1 us (0.69)
  local copies, waits for them, and re-layouts: 6.68 us -> 0 us
  Pallas kernels: 35 us -> 28.9 us
    unnamed x16 -> x0, local copies, waits for them, and re-layouts: 6.68 us -> none
    pallas_call x1, Pallas kernels: 31 us -> 25.5 us  [on_device(): pl.pallas_call(main_kernel, out_shape=(jax.ShapeDtypeStruct((DEV * ROWS *...]
    pallas_call x1, Pallas kernels: 4.01 us -> 3.42 us  [on_device(): pl.pallas_call(place_kernel, out_shape=jax.ShapeDtypeStruct((ROWS, GX * T...]
where the time goes in v3:
time: 29.1 us; the launch traced here: 28.9 us
  Pallas kernels  28.9 us (99%)
    pallas_call x1, Pallas kernels, on_device(): pl.pallas_call(main_kernel, out_shape=(jax.ShapeDtypeStruct((DEV * ROWS *...  25.5 us
    pallas_call x1, Pallas kernels, on_device(): pl.pallas_call(place_kernel, out_shape=jax.ShapeDtypeStruct((ROWS, GX * T...  3.42 us

profile of v3, /device:TPU:1, one launch (start us, length us, event | category | flops | bytes accessed | tf_op | source)
XLA Modules:
  0.0 28.9 jit_solution(8665956605762625696)
XLA Ops:
  0.0 25.5 %main.1 = (f32[1280,1,128]{2,1,0:T(1,128)}, f32[128,1,128]{2,1,0:T(1,128)}) custom-call(bf16[8,32,2048]{2,1,0:T(8,128)(2,1)} %spectra.1, s32[16,128]{1,0:T(8,128)} %bitcast.3, f32[16,128]{1,0:T(8,128)} %bitcast.4, f32[16,128]{1,0:T(8,128)} %bitcast.5, s32[8,32]{1,0:T(8,128)} %surface.1, bf16[16,128,256]{2,1,0:T(8,128)(2,1)} %constant.2.clone.table), custom_call_target="tpu_custom_call" | custom-call | tf_op jit(solution)/shard_map/main/pallas_call | solution.py:260
  25.5 3.4 %place.1 = f32[5,128,256]{2,1,0:T(8,128)} custom-call(f32[1280,1,128]{2,1,0:T(1,128)} %get-tuple-element.7.recv, f32[128,1,128]{2,1,0:T(1,128)} %get-tuple-element.8.sums), custom_call_target="tpu_custom_call" | custom-call | tf_op jit(solution)/shard_map/place/pallas_call | solution.py:294

commit v4 on v3

--- a/solution.py
+++ b/solution.py
@@ -22,7 +22,7 @@
 ROWS = KEEP * BLOCK // DEV
 COUNT = 128 * 256 * KEEP * BLOCK
 MESH = pl.DeviceIdType.MESH
-VMEM_BYTES = 67043328
+VMEM_BYTES = 67043328 - 660 * 1024
 
 
 def base_table():
@@ -87,8 +87,8 @@
 
 
 def main_kernel(
-    spectra, index, weight, phase, surface, table, recv, sums,
-    both, params, idx, surf, tab, hits, x, y, msg, part, load, sem,
+    spectra, index, weight, phase, surface, table, out,
+    both, params, idx, surf, tab, hits, x, y, msg, part, recv, sums, load, sem,
 ):
     f32, bf16 = jnp.float32, jnp.bfloat16
     half = LINES // 2
@@ -131,7 +131,9 @@
         jnp.concatenate([surf[2 * p + q : 2 * p + q + 1, :] for p in range(4)], axis=1)
         for q in range(2)
     ]
-    row = lax.broadcasted_iota(jnp.int32, (NK, 2 * BLOCK), 0)
+    row = lax.broadcasted_iota(jnp.int32, (BLOCK, 2 * BLOCK), 0).astype(jnp.int16)
+    one = jnp.ones((BLOCK, 2 * BLOCK), bf16)
+    zero = jnp.zeros((BLOCK, 2 * BLOCK), bf16)
     nt = (((1,), (1,)), ((), ()))
 
     def compute(q, acc):
@@ -144,7 +146,10 @@
                 pick = jnp.concatenate(
                     [idx[2 * j : 2 * j + 1, :], idx[2 * j + 1 : 2 * j + 2, :]], axis=1
                 )
-                hits[j] = jnp.where(row == pick, 1.0, 0.0).astype(bf16)
+                pick = pick.astype(jnp.int16)
+                for k in range(NK // 128):
+                    seen = row + jnp.int16(128 * k) == pick
+                    hits[j, k * 128 : (k + 1) * 128, :] = jnp.where(seen, one, zero)
             pair = jnp.dot(both[q], hits[j], preferred_element_type=f32)
             for h in range(2):
                 lane = slice(h * BLOCK, (h + 1) * BLOCK)
@@ -227,9 +232,10 @@
     few = sums.at[pl.ds(0, DEV - 1)]
     for ref, s in ((most, 0), (most, 2), (few, 4), (most, 1), (few, 5), (most, 3)):
         pltpu.make_async_copy(ref, ref, sem.at[s]).wait()
-
-
-def place_kernel(recv, sums, out):
+    place(recv, sums, out)
+
+
+def place(recv, sums, out):
     level = jnp.sum(sums[...]) / COUNT + 1e-6
     scale = 1.0 / jnp.full((8, 128), level, jnp.float32)
     lane = lax.broadcasted_iota(jnp.int32, (8, 128), 1) // TY
@@ -257,14 +263,11 @@
     vm = pl.BlockSpec(memory_space=pltpu.VMEM)
     hbm = pl.BlockSpec(memory_space=pltpu.HBM)
     table = jnp.asarray(base_table(), bf16)
-    recv, sums = pl.pallas_call(
+    return pl.pallas_call(
         main_kernel,
-        out_shape=(
-            jax.ShapeDtypeStruct((DEV * ROWS * 2, 1, 128), f32),
-            jax.ShapeDtypeStruct((DEV, 1, 128), f32),
-        ),
+        out_shape=jax.ShapeDtypeStruct((ROWS, GX * TX, GY * TY), f32),
         in_specs=[hbm] * 6,
-        out_specs=[vm] * 2,
+        out_specs=vm,
         scratch_shapes=[
             pltpu.VMEM((2, LINES, NK), bf16),
             pltpu.VMEM((3, RADIX, BLOCK), f32),
@@ -276,6 +279,8 @@
             pltpu.VMEM((RADIX, LINES // 2, 2 * BLOCK), bf16),
             pltpu.VMEM((2 * KEEP * BLOCK, 1, 128), f32),
             pltpu.VMEM((1, 1, 128), f32),
+            pltpu.VMEM((DEV * ROWS * 2, 1, 128), f32),
+            pltpu.VMEM((DEV, 1, 128), f32),
             pltpu.SemaphoreType.DMA((13,)),
             pltpu.SemaphoreType.DMA((9,)),
         ],
@@ -291,14 +296,6 @@
         surface_block,
         table,
     )
-    return pl.pallas_call(
-        place_kernel,
-        out_shape=jax.ShapeDtypeStruct((ROWS, GX * TX, GY * TY), f32),
-        in_specs=[vm] * 2,
-        out_specs=vm,
-        name="place",
-    )(recv, sums)
-
 
 def solution(mesh):
     return jax.shard_map(

time: 29.1 us -> 27.5 us (0.945)
  Pallas kernels: 28.9 us -> 25.3 us
  local copies, waits for them, and re-layouts: 0 us -> 1.99 us
    pallas_call x2 -> x1, Pallas kernels: 28.9 us -> 25.3 us  [on_device(): pl.pallas_call(main_kernel, out_shape=jax.ShapeDtypeStruct((ROWS, GX * TX...]
    unnamed x0 -> x1, local copies, waits for them, and re-layouts: none -> 1.99 us
where the time goes in v4:
time: 27.5 us; the launch traced here: 27.3 us
  Pallas kernels  25.3 us (92%)
  local copies, waits for them, and re-layouts  1.99 us (7%)
    pallas_call x1, Pallas kernels, on_device(): pl.pallas_call(main_kernel, out_shape=jax.ShapeDtypeStruct((ROWS, GX * TX...  25.3 us
    unnamed x1, local copies, waits for them, and re-layouts  1.99 us

profile of v4, /device:TPU:1, one launch (start us, length us, event | category | flops | bytes accessed | tf_op | source)
XLA Modules:
  0.0 27.3 jit_solution(2030106316891882800)
XLA Ops:
  0.0 25.3 %main.1 = f32[5,128,256]{2,1,0:T(8,128)} custom-call(bf16[8,32,2048]{2,1,0:T(8,128)(2,1)} %spectra.1, s32[16,128]{1,0:T(8,128)} %bitcast.3, f32[16,128]{1,0:T(8,128)} %bitcast.4, f32[16,128]{1,0:T(8,128)} %bitcast.5, s32[8,32]{1,0:T(8,128)} %surface.1, bf16[16,128,256]{2,1,0:T(8,128)(2,1)} %constant.2.clone.table), custom_call_target="tpu_custom_call" | custom-call | tf_op jit(solution)/shard_map/main/pallas_call | solution.py:266
  25.3 2.0 %copy.8 = f32[5,128,256]{2,1,0:T(8,128)} copy(f32[5,128,256]{2,1,0:T(8,128)} %main.1) | data formatting | bytes 1310720

commit v5 on v4

--- a/solution.py
+++ b/solution.py
@@ -87,8 +87,8 @@
 
 
 def main_kernel(
-    spectra, index, weight, phase, surface, table, out,
-    both, params, idx, surf, tab, hits, x, y, msg, part, recv, sums, load, sem,
+    spectra, index, weight, phase, surface, table, out, level,
+    both, params, idx, surf, tab, hits, x, y, msg, part, recv, sums, load, sem, groups,
 ):
     f32, bf16 = jnp.float32, jnp.bfloat16
     half = LINES // 2
@@ -197,12 +197,13 @@
         return recv.at[pl.ds((2 * me + q) * ROWS, ROWS)]
 
     def send(q):
+        arrived = sem.at[1] if q == 0 else groups.at[gx]
         for px, py in peers:
             pltpu.make_async_remote_copy(
                 src_ref=slab(q, px * GY + py),
                 dst_ref=landing(q),
                 send_sem=sem.at[2 * q],
-                recv_sem=sem.at[2 * q + 1],
+                recv_sem=arrived,
                 device_id=(px, py),
                 device_id_type=MESH,
             ).start()
@@ -230,31 +231,27 @@
         copy.wait()
     most = recv.at[pl.ds(0, (DEV - 1) * ROWS)]
     few = sums.at[pl.ds(0, DEV - 1)]
-    for ref, s in ((most, 0), (most, 2), (few, 4), (most, 1), (few, 5), (most, 3)):
+    for ref, s in ((most, 0), (most, 2), (few, 4), (most, 1)):
         pltpu.make_async_copy(ref, ref, sem.at[s]).wait()
-    place(recv, sums, out)
-
-
-def place(recv, sums, out):
-    level = jnp.sum(sums[...]) / COUNT + 1e-6
-    scale = 1.0 / jnp.full((8, 128), level, jnp.float32)
     lane = lax.broadcasted_iota(jnp.int32, (8, 128), 1) // TY
     line = lax.broadcasted_iota(jnp.int32, (8, 128), 0) // 2
     step = (line - lane) % 4
-
-    def body(gx, _):
-        x0 = pl.multiple_of(gx * TX, TX)
+    for dz, dy in sorted(itertools.product(range(4), repeat=2), key=lambda o: -hops(o + (0,))):
+        source = zs[-dz % 4] * 4 + ys[-dy % 4]
+        come = GY if dz or dy else GY - 1
+        block = recv.at[pl.ds(0, come * ROWS)]
+        pltpu.make_async_copy(block, block, groups.at[source]).wait()
+        x0 = pl.multiple_of(source * TX, TX)
         for h in range(2):
             for r in range(ROWS):
-                v = recv[pl.ds((gx * GY + 4 * h) * 2 * ROWS + r, 8, stride=ROWS), 0, :]
+                v = recv[pl.ds((source * GY + 4 * h) * 2 * ROWS + r, 8, stride=ROWS), 0, :]
                 w = v
                 for k in range(1, 4):
                     turned = pltpu.roll(pltpu.roll(v, 2 * k, 0), 128 - TY * k, 1)
                     w = jnp.where(step == k, turned, w)
-                out[r, pl.ds(x0, TX), h * 128 : (h + 1) * 128] = jnp.log(1.0 + w * scale)
-        return 0
-
-    lax.fori_loop(0, GX, body, 0, unroll=2)
+                out[r, pl.ds(x0, TX), h * 128 : (h + 1) * 128] = w
+    pltpu.make_async_copy(few, few, sem.at[5]).wait()
+    level[...] = jnp.full((8, 128), jnp.sum(sums[...]) / COUNT + 1e-6, f32)
 
 
 def on_device(spectra, resample_index, resample_weight, disp_phase, surface_block):
@@ -263,11 +260,14 @@
     vm = pl.BlockSpec(memory_space=pltpu.VMEM)
     hbm = pl.BlockSpec(memory_space=pltpu.HBM)
     table = jnp.asarray(base_table(), bf16)
-    return pl.pallas_call(
+    flat, level = pl.pallas_call(
         main_kernel,
-        out_shape=jax.ShapeDtypeStruct((ROWS, GX * TX, GY * TY), f32),
+        out_shape=(
+            jax.ShapeDtypeStruct((ROWS, GX * TX, GY * TY), f32),
+            jax.ShapeDtypeStruct((8, 128), f32),
+        ),
         in_specs=[hbm] * 6,
-        out_specs=vm,
+        out_specs=[vm] * 2,
         scratch_shapes=[
             pltpu.VMEM((2, LINES, NK), bf16),
             pltpu.VMEM((3, RADIX, BLOCK), f32),
@@ -283,6 +283,7 @@
             pltpu.VMEM((DEV, 1, 128), f32),
             pltpu.SemaphoreType.DMA((13,)),
             pltpu.SemaphoreType.DMA((9,)),
+            pltpu.SemaphoreType.DMA((GX,)),
         ],
         compiler_params=pltpu.CompilerParams(
             collective_id=0, has_side_effects=True, vmem_limit_bytes=VMEM_BYTES
@@ -296,6 +297,7 @@
         surface_block,
         table,
     )
+    return jnp.log1p(flat / level[0, 0])
 
 def solution(mesh):
     return jax.shard_map(

time: 27.5 us -> 29.4 us (1.069)
  other arithmetic: 0 us -> 2.78 us
  local copies, waits for them, and re-layouts: 1.99 us -> 1.22 us
    log1p x0 -> x1, other arithmetic: none -> 2.78 us  [on_device(): return jnp.log1p(flat / level[0, 0])]
    unnamed x1 -> x0, local copies, waits for them, and re-layouts: 1.99 us -> none
    slice x0 -> x1, local copies, waits for them, and re-layouts: none -> 1.22 us  [on_device(): return jnp.log1p(flat / level[0, 0])]
where the time goes in v5:
time: 29.4 us; the launch traced here: 29.2 us
  Pallas kernels  25.2 us (86%)
  other arithmetic  2.78 us (9%)
  local copies, waits for them, and re-layouts  1.22 us (4%)
    pallas_call x1, Pallas kernels, on_device(): pl.pallas_call(main_kernel, out_shape=(jax.ShapeDtypeStruct((ROWS, GX * T...  25.2 us
    log1p x1, other arithmetic, on_device(): return jnp.log1p(flat / level[0, 0])  2.78 us
    slice x1, local copies, waits for them, and re-layouts, on_device(): return jnp.log1p(flat / level[0, 0])  1.22 us

profile of v5, /device:TPU:1, one launch (start us, length us, event | category | flops | bytes accessed | tf_op | source)
XLA Modules:
  0.0 29.2 jit_solution(12705779333807443451)
XLA Ops:
  0.0 25.2 %main.1 = (f32[5,128,256]{2,1,0:T(8,128)}, f32[8,128]{1,0:T(8,128)}) custom-call(bf16[8,32,2048]{2,1,0:T(8,128)(2,1)} %spectra.1, s32[16,128]{1,0:T(8,128)} %bitcast.4, f32[16,128]{1,0:T(8,128)} %bitcast.5, f32[16,128]{1,0:T(8,128)} %bitcast.6, s32[8,32]{1,0:T(8,128)} %surface.1, bf16[16,128,256]{2,1,0:T(8,128)(2,1)} %constant.2.clone.table), custom_call_target="tpu_custom_call" | custom-call | tf_op jit(solution)/shard_map/main/pallas_call | solution.py:263
  25.2 1.2 %slice.3 = f32[1,1]{1,0:T(1,128)} slice(f32[8,128]{1,0:T(8,128)} %get-tuple-element.8), slice={[0:1], [0:1]} | slice | bytes 8 | tf_op jit(solution)/shard_map/slice | solution.py:300
  26.4 2.8 %divide_log-plus-one_fusion = f32[5,128,256]{2,1,0:T(8,128)} fusion(f32[5,128,256]{2,1,0:T(8,128)} %get-tuple-element.7, f32[]{:T(128)} %bitcast.3), kind=kLoop, calls=%fused_computation | loop fusion | flops 163840 | bytes 1310724 | tf_op jit(solution)/shard_map/log1p | solution.py:300

commit v6 on v5

--- a/solution.py
+++ b/solution.py
@@ -22,7 +22,7 @@
 ROWS = KEEP * BLOCK // DEV
 COUNT = 128 * 256 * KEEP * BLOCK
 MESH = pl.DeviceIdType.MESH
-VMEM_BYTES = 67043328 - 660 * 1024
+VMEM_BYTES = 67043328
 
 
 def base_table():
@@ -65,15 +65,11 @@
     return a[0] - b[0], a[1] - b[1]
 
 
-def fft(z):
-    n = len(z)
-    if n == 1:
-        return z
-    even, odd = fft(z[0::2]), fft(z[1::2])
-    odd = [rot(odd[k], k, n) for k in range(n // 2)]
-    return [add(even[k], odd[k]) for k in range(n // 2)] + [
-        sub(even[k], odd[k]) for k in range(n // 2)
-    ]
+def fft4(z):
+    a, b = add(z[0], z[2]), sub(z[0], z[2])
+    c, d = add(z[1], z[3]), sub(z[1], z[3])
+    d = rot(d, 1, 4)
+    return [add(a, c), add(b, d), sub(a, c), sub(b, d)]
 
 
 def hops(o):
@@ -87,8 +83,8 @@
 
 
 def main_kernel(
-    spectra, index, weight, phase, surface, table, out, level,
-    both, params, idx, surf, tab, hits, x, y, msg, part, recv, sums, load, sem, groups,
+    spectra, index, weight, phase, surface, table, out,
+    both, params, idx, surf, tab, hits, x, mid, y, msg, part, recv, sums, placed, load, sem, groups,
 ):
     f32, bf16 = jnp.float32, jnp.bfloat16
     half = LINES // 2
@@ -141,53 +137,55 @@
             copy.wait()
         lines = both[q, :half, :]
         both[q, half:, :] = jnp.concatenate([lines[:, 1:], lines[:, :1]], axis=1)
-        for j in range(RADIX // 2):
-            if q == 0:
-                pick = jnp.concatenate(
-                    [idx[2 * j : 2 * j + 1, :], idx[2 * j + 1 : 2 * j + 2, :]], axis=1
-                )
-                pick = pick.astype(jnp.int16)
-                for k in range(NK // 128):
-                    seen = row + jnp.int16(128 * k) == pick
-                    hits[j, k * 128 : (k + 1) * 128, :] = jnp.where(seen, one, zero)
-            pair = jnp.dot(both[q], hits[j], preferred_element_type=f32)
-            for h in range(2):
-                lane = slice(h * BLOCK, (h + 1) * BLOCK)
-                w = params[0, 2 * j + h : 2 * j + h + 1, :]
-                x[2 * j + h] = (1.0 - w) * pair[:half, lane] + w * pair[half:, lane]
-
-        def spread(g, _):
-            r0 = pl.multiple_of(g * 16, 16)
-            parts = []
-            for n in range(RADIX):
-                v = x[n, pl.ds(r0, 16), :]
-                parts.append(
-                    [
-                        (v * params[1 + o, n : n + 1, :]).astype(bf16).astype(f32)
-                        for o in range(2)
-                    ]
-                )
-            low = fft([(re[:8], im[:8]) for re, im in parts])
-            high = fft([(re[8:], im[8:]) for re, im in parts])
-            for c in range(RADIX):
-                for o in range(2):
-                    rows = jnp.concatenate([low[c][o], high[c][o]], axis=0)
-                    y[c, pl.ds(r0, 16), o * BLOCK : (o + 1) * BLOCK] = rows.astype(bf16)
-            return 0
-
-        lax.fori_loop(0, half // 16, spread, 0)
+        for n in range(4):
+            for e in range(2):
+                if q == 0:
+                    pick = jnp.concatenate(
+                        [idx[n + 8 * e + 4 * h : n + 8 * e + 4 * h + 1, :] for h in range(2)], axis=1
+                    ).astype(jnp.int16)
+                    for k in range(NK // 128):
+                        seen = row + jnp.int16(128 * k) == pick
+                        hits[2 * n + e, k * 128 : (k + 1) * 128, :] = jnp.where(seen, one, zero)
+                pair = jnp.dot(both[q], hits[2 * n + e], preferred_element_type=f32)
+                for h in range(2):
+                    at = n + 8 * e + 4 * h
+                    lane = slice(h * BLOCK, (h + 1) * BLOCK)
+                    w = params[0, at : at + 1, :]
+                    x[at] = (1.0 - w) * pair[:half, lane] + w * pair[half:, lane]
+            for g in range(half // 16):
+                rows = slice(16 * g, 16 * g + 16)
+                z = []
+                for m in range(4):
+                    at = n + 4 * m
+                    v = x[at, rows, :]
+                    z.append(
+                        [
+                            (v * params[1 + o, at : at + 1, :]).astype(bf16).astype(f32)
+                            for o in range(2)
+                        ]
+                    )
+                for c, value in enumerate(fft4(z)):
+                    for o, half_value in enumerate(rot(value, n * c, RADIX)):
+                        mid[n, c, o, rows, :] = half_value
         if q == 0:
             big.wait()
-        for c in range(RADIX):
-            depth = lax.dot_general(tab[c], y[c], nt, preferred_element_type=f32)
-            power = depth[:64] * depth[:64] + depth[64:] * depth[64:]
-            tile = [power[8 * b : 8 * b + 8] for b in range(8)]
-            for k in range(KEEP):
-                kept = tile[k]
-                for s in range(1, 4):
-                    kept = jnp.where(tops[q] == s, tile[k + s], kept)
-                acc = acc + kept
-                msg[pl.ds((q * KEEP + k) * BLOCK + c, 8, stride=RADIX), 0, :] = kept
+        for low in range(4):
+            for g in range(half // 16):
+                rows = slice(16 * g, 16 * g + 16)
+                z = [[mid[n, low, o, rows, :] for o in range(2)] for n in range(4)]
+                for high, value in enumerate(fft4(z)):
+                    for o in range(2):
+                        y[low + 4 * high, rows, o * BLOCK : (o + 1) * BLOCK] = value[o].astype(bf16)
+            for c in range(low, RADIX, 4):
+                depth = lax.dot_general(tab[c], y[c], nt, preferred_element_type=f32)
+                power = depth[:64] * depth[:64] + depth[64:] * depth[64:]
+                tile = [power[8 * b : 8 * b + 8] for b in range(8)]
+                for k in range(KEEP):
+                    kept = tile[k]
+                    for s in range(1, 4):
+                        kept = jnp.where(tops[q] == s, tile[k + s], kept)
+                    acc = acc + kept
+                    msg[pl.ds((q * KEEP + k) * BLOCK + c, 8, stride=RADIX), 0, :] = kept
         return acc
 
     def slab(q, dest):
@@ -231,8 +229,10 @@
         copy.wait()
     most = recv.at[pl.ds(0, (DEV - 1) * ROWS)]
     few = sums.at[pl.ds(0, DEV - 1)]
-    for ref, s in ((most, 0), (most, 2), (few, 4), (most, 1)):
+    for ref, s in ((most, 0), (most, 2), (few, 4), (few, 5), (most, 1)):
         pltpu.make_async_copy(ref, ref, sem.at[s]).wait()
+    level = jnp.sum(sums[...]) / COUNT + 1e-6
+    scale = 1.0 / jnp.full((8, 128), level, f32)
     lane = lax.broadcasted_iota(jnp.int32, (8, 128), 1) // TY
     line = lax.broadcasted_iota(jnp.int32, (8, 128), 0) // 2
     step = (line - lane) % 4
@@ -249,25 +249,24 @@
                 for k in range(1, 4):
                     turned = pltpu.roll(pltpu.roll(v, 2 * k, 0), 128 - TY * k, 1)
                     w = jnp.where(step == k, turned, w)
-                out[r, pl.ds(x0, TX), h * 128 : (h + 1) * 128] = w
-    pltpu.make_async_copy(few, few, sem.at[5]).wait()
-    level[...] = jnp.full((8, 128), jnp.sum(sums[...]) / COUNT + 1e-6, f32)
+                placed[r, pl.ds(x0, TX), h * 128 : (h + 1) * 128] = jnp.log(1.0 + w * scale)
+        gone = pltpu.make_async_copy(
+            placed.at[:, pl.ds(x0, TX)], out.at[:, pl.ds(x0, TX)], sem.at[9]
+        )
+        gone.start()
+    pltpu.make_async_copy(placed, out, sem.at[9]).wait()
 
 
 def on_device(spectra, resample_index, resample_weight, disp_phase, surface_block):
     f32 = jnp.float32
     bf16 = jnp.bfloat16
-    vm = pl.BlockSpec(memory_space=pltpu.VMEM)
     hbm = pl.BlockSpec(memory_space=pltpu.HBM)
     table = jnp.asarray(base_table(), bf16)
-    flat, level = pl.pallas_call(
+    return pl.pallas_call(
         main_kernel,
-        out_shape=(
-            jax.ShapeDtypeStruct((ROWS, GX * TX, GY * TY), f32),
-            jax.ShapeDtypeStruct((8, 128), f32),
-        ),
+        out_shape=jax.ShapeDtypeStruct((ROWS, GX * TX, GY * TY), f32),
         in_specs=[hbm] * 6,
-        out_specs=[vm] * 2,
+        out_specs=hbm,
         scratch_shapes=[
             pltpu.VMEM((2, LINES, NK), bf16),
             pltpu.VMEM((3, RADIX, BLOCK), f32),
@@ -276,13 +275,15 @@
             pltpu.VMEM((RADIX, BLOCK, 2 * BLOCK), bf16),
             pltpu.VMEM((RADIX // 2, NK, 2 * BLOCK), bf16),
             pltpu.VMEM((RADIX, LINES // 2, BLOCK), f32),
+            pltpu.VMEM((4, 4, 2, LINES // 2, BLOCK), f32),
             pltpu.VMEM((RADIX, LINES // 2, 2 * BLOCK), bf16),
             pltpu.VMEM((2 * KEEP * BLOCK, 1, 128), f32),
             pltpu.VMEM((1, 1, 128), f32),
             pltpu.VMEM((DEV * ROWS * 2, 1, 128), f32),
             pltpu.VMEM((DEV, 1, 128), f32),
+            pltpu.VMEM((ROWS, GX * TX, GY * TY), f32),
             pltpu.SemaphoreType.DMA((13,)),
-            pltpu.SemaphoreType.DMA((9,)),
+            pltpu.SemaphoreType.DMA((10,)),
             pltpu.SemaphoreType.DMA((GX,)),
         ],
         compiler_params=pltpu.CompilerParams(
@@ -297,7 +298,6 @@
         surface_block,
         table,
     )
-    return jnp.log1p(flat / level[0, 0])
 
 def solution(mesh):
     return jax.shard_map(

time: 29.4 us -> 26.6 us (0.905)
  other arithmetic: 2.78 us -> 0 us
  Pallas kernels: 25.2 us -> 24.4 us
  local copies, waits for them, and re-layouts: 1.22 us -> 1.99 us
    log1p x1 -> x0, other arithmetic: 2.78 us -> none  [on_device(): return jnp.log1p(flat / level[0, 0])]
    unnamed x0 -> x1, local copies, waits for them, and re-layouts: none -> 1.99 us
    slice x1 -> x0, local copies, waits for them, and re-layouts: 1.22 us -> none  [on_device(): return jnp.log1p(flat / level[0, 0])]
    pallas_call x1, Pallas kernels: 25.2 us -> 24.4 us  [on_device(): pl.pallas_call(main_kernel, out_shape=jax.ShapeDtypeStruct((ROWS, GX * TX...]
where the time goes in v6:
time: 26.6 us; the launch traced here: 26.4 us
  Pallas kernels  24.4 us (92%)
  local copies, waits for them, and re-layouts  1.99 us (7%)
    pallas_call x1, Pallas kernels, on_device(): pl.pallas_call(main_kernel, out_shape=jax.ShapeDtypeStruct((ROWS, GX * TX...  24.4 us
    unnamed x1, local copies, waits for them, and re-layouts  1.99 us

profile of v6, /device:TPU:1, one launch (start us, length us, event | category | flops | bytes accessed | tf_op | source)
XLA Modules:
  0.0 26.4 jit_solution(7456329637050432242)
XLA Ops:
  0.0 24.4 %main.1 = f32[5,128,256]{2,1,0:T(8,128)} custom-call(bf16[8,32,2048]{2,1,0:T(8,128)(2,1)} %spectra.1, s32[16,128]{1,0:T(8,128)} %bitcast.3, f32[16,128]{1,0:T(8,128)} %bitcast.4, f32[16,128]{1,0:T(8,128)} %bitcast.5, s32[8,32]{1,0:T(8,128)} %surface.1, bf16[16,128,256]{2,1,0:T(8,128)(2,1)} %constant.2.clone.table), custom_call_target="tpu_custom_call" | custom-call | tf_op jit(solution)/shard_map/main/pallas_call | solution.py:265
  24.4 2.0 %copy.8 = f32[5,128,256]{2,1,0:T(8,128)} copy(f32[5,128,256]{2,1,0:T(8,128)} %main.1) | data formatting | bytes 1310720

commit v7 on v6

--- a/solution.py
+++ b/solution.py
@@ -185,7 +185,7 @@
                     for s in range(1, 4):
                         kept = jnp.where(tops[q] == s, tile[k + s], kept)
                     acc = acc + kept
-                    msg[pl.ds((q * KEEP + k) * BLOCK + c, 8, stride=RADIX), 0, :] = kept
+                    msg[pl.ds((q * KEEP + k) * BLOCK + c, 8, stride=RADIX), :] = kept
         return acc
 
     def slab(q, dest):
@@ -236,24 +236,25 @@
     lane = lax.broadcasted_iota(jnp.int32, (8, 128), 1) // TY
     line = lax.broadcasted_iota(jnp.int32, (8, 128), 0) // 2
     step = (line - lane) % 4
-    for dz, dy in sorted(itertools.product(range(4), repeat=2), key=lambda o: -hops(o + (0,))):
-        source = zs[-dz % 4] * 4 + ys[-dy % 4]
-        come = GY if dz or dy else GY - 1
-        block = recv.at[pl.ds(0, come * ROWS)]
-        pltpu.make_async_copy(block, block, groups.at[source]).wait()
-        x0 = pl.multiple_of(source * TX, TX)
-        for h in range(2):
-            for r in range(ROWS):
-                v = recv[pl.ds((source * GY + 4 * h) * 2 * ROWS + r, 8, stride=ROWS), 0, :]
-                w = v
-                for k in range(1, 4):
-                    turned = pltpu.roll(pltpu.roll(v, 2 * k, 0), 128 - TY * k, 1)
-                    w = jnp.where(step == k, turned, w)
-                placed[r, pl.ds(x0, TX), h * 128 : (h + 1) * 128] = jnp.log(1.0 + w * scale)
-        gone = pltpu.make_async_copy(
-            placed.at[:, pl.ds(x0, TX)], out.at[:, pl.ds(x0, TX)], sem.at[9]
-        )
-        gone.start()
+    around = sorted(itertools.product(range(4), repeat=2), key=lambda o: -hops(o + (0,)))
+    for batch in (around[:5], around[5:11], around[11:]):
+        sources = [zs[-dz % 4] * 4 + ys[-dy % 4] for dz, dy in batch]
+        for (dz, dy), source in zip(batch, sources):
+            block = recv.at[pl.ds(0, (GY if dz or dy else GY - 1) * ROWS)]
+            pltpu.make_async_copy(block, block, groups.at[source]).wait()
+        for source in sources:
+            x0 = pl.multiple_of(source * TX, TX)
+            for h in range(2):
+                for r in range(ROWS):
+                    v = recv[pl.ds((source * GY + 4 * h) * 2 * ROWS + r, 8, stride=ROWS), :]
+                    w = v
+                    for k in range(1, 4):
+                        turned = pltpu.roll(pltpu.roll(v, 2 * k, 0), 128 - TY * k, 1)
+                        w = jnp.where(step == k, turned, w)
+                    placed[r, pl.ds(x0, TX), h * 128 : (h + 1) * 128] = jnp.log(1.0 + w * scale)
+            pltpu.make_async_copy(
+                placed.at[:, pl.ds(x0, TX)], out.at[:, pl.ds(x0, TX)], sem.at[9]
+            ).start()
     pltpu.make_async_copy(placed, out, sem.at[9]).wait()
 
 
@@ -277,9 +278,9 @@
             pltpu.VMEM((RADIX, LINES // 2, BLOCK), f32),
             pltpu.VMEM((4, 4, 2, LINES // 2, BLOCK), f32),
             pltpu.VMEM((RADIX, LINES // 2, 2 * BLOCK), bf16),
-            pltpu.VMEM((2 * KEEP * BLOCK, 1, 128), f32),
+            pltpu.VMEM((2 * KEEP * BLOCK, 128), f32),
             pltpu.VMEM((1, 1, 128), f32),
-            pltpu.VMEM((DEV * ROWS * 2, 1, 128), f32),
+            pltpu.VMEM((DEV * ROWS * 2, 128), f32),
             pltpu.VMEM((DEV, 1, 128), f32),
             pltpu.VMEM((ROWS, GX * TX, GY * TY), f32),
             pltpu.SemaphoreType.DMA((13,)),

time: 26.6 us -> 25.7 us (0.966)
  Pallas kernels: 24.4 us -> 23.5 us
    pallas_call x1, Pallas kernels: 24.4 us -> 23.5 us  [on_device(): pl.pallas_call(main_kernel, out_shape=jax.ShapeDtypeStruct((ROWS, GX * TX...]
where the time goes in v7:
time: 25.7 us; the launch traced here: 25.5 us
  Pallas kernels  23.5 us (91%)
  local copies, waits for them, and re-layouts  1.99 us (8%)
    pallas_call x1, Pallas kernels, on_device(): pl.pallas_call(main_kernel, out_shape=jax.ShapeDtypeStruct((ROWS, GX * TX...  23.5 us
    unnamed x1, local copies, waits for them, and re-layouts  1.99 us

profile of v7, /device:TPU:1, one launch (start us, length us, event | category | flops | bytes accessed | tf_op | source)
XLA Modules:
  0.0 25.5 jit_solution(9254226034649928315)
XLA Ops:
  0.0 23.5 %main.1 = f32[5,128,256]{2,1,0:T(8,128)} custom-call(bf16[8,32,2048]{2,1,0:T(8,128)(2,1)} %spectra.1, s32[16,128]{1,0:T(8,128)} %bitcast.3, f32[16,128]{1,0:T(8,128)} %bitcast.4, f32[16,128]{1,0:T(8,128)} %bitcast.5, s32[8,32]{1,0:T(8,128)} %surface.1, bf16[16,128,256]{2,1,0:T(8,128)(2,1)} %constant.2.clone.table), custom_call_target="tpu_custom_call" | custom-call | tf_op jit(solution)/shard_map/main/pallas_call | solution.py:266
  23.5 2.0 %copy.8 = f32[5,128,256]{2,1,0:T(8,128)} copy(f32[5,128,256]{2,1,0:T(8,128)} %main.1) | data formatting | bytes 1310720

commit v8 on v7

--- a/solution.py
+++ b/solution.py
@@ -23,6 +23,7 @@
 COUNT = 128 * 256 * KEEP * BLOCK
 MESH = pl.DeviceIdType.MESH
 VMEM_BYTES = 67043328
+FAR = 64
 
 
 def base_table():
@@ -84,7 +85,7 @@
 
 def main_kernel(
     spectra, index, weight, phase, surface, table, out,
-    both, params, idx, surf, tab, hits, x, mid, y, msg, part, recv, sums, placed, load, sem, groups,
+    both, params, idx, surf, tab, hits, x, mid, y, msg, part, row_part, recv, row_sums, sums, placed, load, sem, groups,
 ):
     f32, bf16 = jnp.float32, jnp.bfloat16
     half = LINES // 2
@@ -133,8 +134,6 @@
     nt = (((1,), (1,)), ((), ()))
 
     def compute(q, acc):
-        for copy in tiles[4 * q : 4 * q + 4]:
-            copy.wait()
         lines = both[q, :half, :]
         both[q, half:, :] = jnp.concatenate([lines[:, 1:], lines[:, :1]], axis=1)
         for n in range(4):
@@ -194,9 +193,9 @@
     def landing(q):
         return recv.at[pl.ds((2 * me + q) * ROWS, ROWS)]
 
-    def send(q):
+    def send(q, among):
         arrived = sem.at[1] if q == 0 else groups.at[gx]
-        for px, py in peers:
+        for px, py in among:
             pltpu.make_async_remote_copy(
                 src_ref=slab(q, px * GY + py),
                 dst_ref=landing(q),
@@ -206,36 +205,58 @@
                 device_id_type=MESH,
             ).start()
 
+    def share(source, target, s, among):
+        for to in among:
+            pltpu.make_async_remote_copy(
+                src_ref=source,
+                dst_ref=target,
+                send_sem=sem.at[s],
+                recv_sem=sem.at[s + 1],
+                device_id=to,
+                device_id_type=MESH,
+            ).start()
+
+    for copy in tiles[:4]:
+        copy.wait()
     acc = compute(0, jnp.zeros((8, 128), f32))
+    for copy in tiles[4:]:
+        copy.wait()
     pl.semaphore_wait(barrier, DEV - 1)
-    send(0)
+    send(0, peers)
     acc = compute(1, acc)
     part[...] = jnp.sum(acc, axis=0, keepdims=True).reshape(1, 1, 128)
-    for px, py in peers:
-        pltpu.make_async_remote_copy(
-            src_ref=part,
-            dst_ref=sums.at[pl.ds(me, 1)],
-            send_sem=sem.at[4],
-            recv_sem=sem.at[5],
-            device_id=(px, py),
-            device_id_type=MESH,
-        ).start()
-    send(1)
-    own = [pltpu.make_async_copy(slab(q, me), landing(q), sem.at[6 + q]) for q in range(2)]
-    own.append(pltpu.make_async_copy(part, sums.at[pl.ds(me, 1)], sem.at[8]))
+    row_peers = [to for o, to in zip(OFFSETS, peers) if not any(o[:2])]
+    column_peers = [to for o, to in zip(OFFSETS, peers) if not any(o[2:])]
+    send(1, peers[:8])
+    share(part, row_sums.at[pl.ds(gy, 1)], 4, row_peers)
+    own = [
+        pltpu.make_async_copy(part, row_sums.at[pl.ds(gy, 1)], sem.at[8]),
+        pltpu.make_async_copy(slab(0, me), landing(0), sem.at[6]),
+        pltpu.make_async_copy(slab(1, me), landing(1), sem.at[7]),
+    ]
     for copy in own:
         copy.start()
-    for copy in own:
+    send(1, peers[8:FAR])
+    own[0].wait()
+    few = row_sums.at[pl.ds(0, GY - 1)]
+    pltpu.make_async_copy(few, few, sem.at[5]).wait()
+    row_part[...] = jnp.sum(row_sums[...], axis=0, keepdims=True)
+    send(1, peers[FAR : FAR + 8])
+    share(row_part, sums.at[pl.ds(gx, 1)], 10, column_peers)
+    own.append(pltpu.make_async_copy(row_part, sums.at[pl.ds(gx, 1)], sem.at[12]))
+    own[-1].start()
+    send(1, peers[FAR + 8 :])
+    for copy in own[1:]:
         copy.wait()
     most = recv.at[pl.ds(0, (DEV - 1) * ROWS)]
-    few = sums.at[pl.ds(0, DEV - 1)]
-    for ref, s in ((most, 0), (most, 2), (few, 4), (few, 5), (most, 1)):
+    line = sums.at[pl.ds(0, GX - 1)]
+    for ref, s in ((most, 0), (most, 2), (few, 4), (line, 10), (line, 11), (most, 1)):
         pltpu.make_async_copy(ref, ref, sem.at[s]).wait()
     level = jnp.sum(sums[...]) / COUNT + 1e-6
     scale = 1.0 / jnp.full((8, 128), level, f32)
     lane = lax.broadcasted_iota(jnp.int32, (8, 128), 1) // TY
-    line = lax.broadcasted_iota(jnp.int32, (8, 128), 0) // 2
-    step = (line - lane) % 4
+    pair = lax.broadcasted_iota(jnp.int32, (8, 128), 0) // 2
+    step = (pair - lane) % 4
     around = sorted(itertools.product(range(4), repeat=2), key=lambda o: -hops(o + (0,)))
     for batch in (around[:5], around[5:11], around[11:]):
         sources = [zs[-dz % 4] * 4 + ys[-dy % 4] for dz, dy in batch]
@@ -280,11 +301,13 @@
             pltpu.VMEM((RADIX, LINES // 2, 2 * BLOCK), bf16),
             pltpu.VMEM((2 * KEEP * BLOCK, 128), f32),
             pltpu.VMEM((1, 1, 128), f32),
+            pltpu.VMEM((1, 1, 128), f32),
             pltpu.VMEM((DEV * ROWS * 2, 128), f32),
-            pltpu.VMEM((DEV, 1, 128), f32),
+            pltpu.VMEM((GY, 1, 128), f32),
+            pltpu.VMEM((GX, 1, 128), f32),
             pltpu.VMEM((ROWS, GX * TX, GY * TY), f32),
             pltpu.SemaphoreType.DMA((13,)),
-            pltpu.SemaphoreType.DMA((10,)),
+            pltpu.SemaphoreType.DMA((13,)),
             pltpu.SemaphoreType.DMA((GX,)),
         ],
         compiler_params=pltpu.CompilerParams(

time: 25.7 us -> 26.4 us (1.027)
  Pallas kernels: 23.5 us -> 24.2 us
    pallas_call x1, Pallas kernels: 23.5 us -> 24.2 us  [on_device(): pl.pallas_call(main_kernel, out_shape=jax.ShapeDtypeStruct((ROWS, GX * TX...]
where the time goes in v8:
time: 26.4 us; the launch traced here: 26.2 us
  Pallas kernels  24.2 us (92%)
  local copies, waits for them, and re-layouts  1.99 us (8%)
    pallas_call x1, Pallas kernels, on_device(): pl.pallas_call(main_kernel, out_shape=jax.ShapeDtypeStruct((ROWS, GX * TX...  24.2 us
    unnamed x1, local copies, waits for them, and re-layouts  1.99 us

profile of v8, /device:TPU:1, one launch (start us, length us, event | category | flops | bytes accessed | tf_op | source)
XLA Modules:
  0.0 26.2 jit_solution(7119365056624507339)
XLA Ops:
  0.0 24.2 %main.1 = f32[5,128,256]{2,1,0:T(8,128)} custom-call(bf16[8,32,2048]{2,1,0:T(8,128)(2,1)} %spectra.1, s32[16,128]{1,0:T(8,128)} %bitcast.3, f32[16,128]{1,0:T(8,128)} %bitcast.4, f32[16,128]{1,0:T(8,128)} %bitcast.5, s32[8,32]{1,0:T(8,128)} %surface.1, bf16[16,128,256]{2,1,0:T(8,128)(2,1)} %constant.2.clone.table), custom_call_target="tpu_custom_call" | custom-call | tf_op jit(solution)/shard_map/main/pallas_call | solution.py:287
  24.2 2.0 %copy.8 = f32[5,128,256]{2,1,0:T(8,128)} copy(f32[5,128,256]{2,1,0:T(8,128)} %main.1) | data formatting | bytes 1310720

commit v9 on v7

--- a/solution.py
+++ b/solution.py
@@ -21,7 +21,7 @@
 LINES = TX * TY
 ROWS = KEEP * BLOCK // DEV
 COUNT = 128 * 256 * KEEP * BLOCK
-MESH = pl.DeviceIdType.MESH
+FLAT = pl.DeviceIdType.LOGICAL
 VMEM_BYTES = 67043328
 
 
@@ -84,7 +84,7 @@
 
 def main_kernel(
     spectra, index, weight, phase, surface, table, out,
-    both, params, idx, surf, tab, hits, x, mid, y, msg, part, recv, sums, placed, load, sem, groups,
+    both, params, idx, surf, tab, hits, x, mid, y, msg, part, halves, recv, sums, placed, load, sem, groups,
 ):
     f32, bf16 = jnp.float32, jnp.bfloat16
     half = LINES // 2
@@ -94,9 +94,12 @@
     ys = [(gx % 4 + d) % 4 for d in range(4)]
     xs = [(gy // 2 + d) % 4 for d in range(4)]
     cs = [(gy % 2 + d) % 2 for d in range(2)]
-    zy = [[z * 4 + v for v in ys] for z in zs]
+    zy = [[(z * 4 + v) * GY for v in ys] for z in zs]
     xc = [[v * 2 + c for c in cs] for v in xs]
-    peers = [(zy[o[0]][o[1]], xc[o[2]][o[3]]) for o in OFFSETS]
+    peers = [zy[o[0]][o[1]] + xc[o[2]][o[3]] for o in OFFSETS]
+    alike = [to for o, to in zip(OFFSETS, peers) if o[3] == 0]
+    partner = zy[0][0] + xc[0][1]
+    chip = gx * (GY // 2) + gy // 2
     barrier = pltpu.get_barrier_semaphore()
 
     small = [
@@ -116,7 +119,7 @@
     for copy in small + tiles + [big]:
         copy.start()
     for to in peers:
-        pl.semaphore_signal(barrier, inc=1, device_id=to, device_id_type=MESH)
+        pl.semaphore_signal(barrier, inc=1, device_id=to, device_id_type=FLAT)
     for copy in small:
         copy.wait()
     cosp = jnp.cos(params[1])
@@ -132,11 +135,13 @@
     zero = jnp.zeros((BLOCK, 2 * BLOCK), bf16)
     nt = (((1,), (1,)), ((), ()))
 
-    def compute(q, acc):
+    def shift(q):
         for copy in tiles[4 * q : 4 * q + 4]:
             copy.wait()
         lines = both[q, :half, :]
         both[q, half:, :] = jnp.concatenate([lines[:, 1:], lines[:, :1]], axis=1)
+
+    def compute(q, acc):
         for n in range(4):
             for e in range(2):
                 if q == 0:
@@ -194,44 +199,59 @@
     def landing(q):
         return recv.at[pl.ds((2 * me + q) * ROWS, ROWS)]
 
-    def send(q):
+    def send(q, among):
         arrived = sem.at[1] if q == 0 else groups.at[gx]
-        for px, py in peers:
+        for to in among:
             pltpu.make_async_remote_copy(
-                src_ref=slab(q, px * GY + py),
+                src_ref=slab(q, to),
                 dst_ref=landing(q),
                 send_sem=sem.at[2 * q],
                 recv_sem=arrived,
-                device_id=(px, py),
-                device_id_type=MESH,
+                device_id=to,
+                device_id_type=FLAT,
             ).start()
 
+    shift(0)
     acc = compute(0, jnp.zeros((8, 128), f32))
+    shift(1)
     pl.semaphore_wait(barrier, DEV - 1)
-    send(0)
+    send(0, peers)
     acc = compute(1, acc)
     part[...] = jnp.sum(acc, axis=0, keepdims=True).reshape(1, 1, 128)
-    for px, py in peers:
+    send(1, peers[:8])
+    for to in alike:
         pltpu.make_async_remote_copy(
             src_ref=part,
-            dst_ref=sums.at[pl.ds(me, 1)],
+            dst_ref=sums.at[pl.ds(chip, 1)],
             send_sem=sem.at[4],
             recv_sem=sem.at[5],
-            device_id=(px, py),
-            device_id_type=MESH,
+            device_id=to,
+            device_id_type=FLAT,
         ).start()
-    send(1)
+    send(1, peers[8:])
     own = [pltpu.make_async_copy(slab(q, me), landing(q), sem.at[6 + q]) for q in range(2)]
-    own.append(pltpu.make_async_copy(part, sums.at[pl.ds(me, 1)], sem.at[8]))
+    own.append(pltpu.make_async_copy(part, sums.at[pl.ds(chip, 1)], sem.at[8]))
     for copy in own:
         copy.start()
     for copy in own:
         copy.wait()
     most = recv.at[pl.ds(0, (DEV - 1) * ROWS)]
-    few = sums.at[pl.ds(0, DEV - 1)]
-    for ref, s in ((most, 0), (most, 2), (few, 4), (few, 5), (most, 1)):
+    few = sums.at[pl.ds(0, DEV // 2 - 1)]
+    pltpu.make_async_copy(few, few, sem.at[5]).wait()
+    halves[0] = jnp.sum(sums[...], axis=0)
+    for ref, s in ((most, 0), (most, 2), (few, 4), (most, 1)):
         pltpu.make_async_copy(ref, ref, sem.at[s]).wait()
-    level = jnp.sum(sums[...]) / COUNT + 1e-6
+    swap = pltpu.make_async_remote_copy(
+        src_ref=halves.at[0],
+        dst_ref=halves.at[1],
+        send_sem=sem.at[10],
+        recv_sem=sem.at[11],
+        device_id=partner,
+        device_id_type=FLAT,
+    )
+    swap.start()
+    swap.wait()
+    level = jnp.sum(halves[...]) / COUNT + 1e-6
     scale = 1.0 / jnp.full((8, 128), level, f32)
     lane = lax.broadcasted_iota(jnp.int32, (8, 128), 1) // TY
     line = lax.broadcasted_iota(jnp.int32, (8, 128), 0) // 2
@@ -280,11 +300,12 @@
             pltpu.VMEM((RADIX, LINES // 2, 2 * BLOCK), bf16),
             pltpu.VMEM((2 * KEEP * BLOCK, 128), f32),
             pltpu.VMEM((1, 1, 128), f32),
+            pltpu.VMEM((2, 1, 128), f32),
             pltpu.VMEM((DEV * ROWS * 2, 128), f32),
-            pltpu.VMEM((DEV, 1, 128), f32),
+            pltpu.VMEM((DEV // 2, 1, 128), f32),
             pltpu.VMEM((ROWS, GX * TX, GY * TY), f32),
             pltpu.SemaphoreType.DMA((13,)),
-            pltpu.SemaphoreType.DMA((10,)),
+            pltpu.SemaphoreType.DMA((12,)),
             pltpu.SemaphoreType.DMA((GX,)),
         ],
         compiler_params=pltpu.CompilerParams(

time: 25.7 us -> 26 us (1.012)
  Pallas kernels: 23.5 us -> 23.8 us
    pallas_call x1, Pallas kernels: 23.5 us -> 23.8 us  [on_device(): pl.pallas_call(main_kernel, out_shape=jax.ShapeDtypeStruct((ROWS, GX * TX...]
where the time goes in v9:
time: 26 us; the launch traced here: 25.8 us
  Pallas kernels  23.8 us (92%)
  local copies, waits for them, and re-layouts  1.99 us (8%)
    pallas_call x1, Pallas kernels, on_device(): pl.pallas_call(main_kernel, out_shape=jax.ShapeDtypeStruct((ROWS, GX * TX...  23.8 us
    unnamed x1, local copies, waits for them, and re-layouts  1.99 us

profile of v9, /device:TPU:1, one launch (start us, length us, event | category | flops | bytes accessed | tf_op | source)
XLA Modules:
  0.0 25.8 jit_solution(7301251535096527310)
XLA Ops:
  0.0 23.8 %main.1 = f32[5,128,256]{2,1,0:T(8,128)} custom-call(bf16[8,32,2048]{2,1,0:T(8,128)(2,1)} %spectra.1, s32[16,128]{1,0:T(8,128)} %bitcast.3, f32[16,128]{1,0:T(8,128)} %bitcast.4, f32[16,128]{1,0:T(8,128)} %bitcast.5, s32[8,32]{1,0:T(8,128)} %surface.1, bf16[16,128,256]{2,1,0:T(8,128)(2,1)} %constant.2.clone.table), custom_call_target="tpu_custom_call" | custom-call | tf_op jit(solution)/shard_map/main/pallas_call | solution.py:286
  23.8 2.0 %copy.8 = f32[5,128,256]{2,1,0:T(8,128)} copy(f32[5,128,256]{2,1,0:T(8,128)} %main.1) | data formatting | bytes 1310720

commit v10 on v9

--- a/solution.py
+++ b/solution.py
@@ -21,8 +21,9 @@
 LINES = TX * TY
 ROWS = KEEP * BLOCK // DEV
 COUNT = 128 * 256 * KEEP * BLOCK
-FLAT = pl.DeviceIdType.LOGICAL
+MESH = pl.DeviceIdType.MESH
 VMEM_BYTES = 67043328
+CHUNKS = 8
 
 
 def base_table():
@@ -83,8 +84,8 @@
 
 
 def main_kernel(
-    spectra, index, weight, phase, surface, table, out,
-    both, params, idx, surf, tab, hits, x, mid, y, msg, part, halves, recv, sums, placed, load, sem, groups,
+    spectra, index, weight, phase, surface, table, recv, totals,
+    both, params, idx, surf, tab, hits, x, mid, y, msg, part, total, sums, load, sem,
 ):
     f32, bf16 = jnp.float32, jnp.bfloat16
     half = LINES // 2
@@ -94,11 +95,11 @@
     ys = [(gx % 4 + d) % 4 for d in range(4)]
     xs = [(gy // 2 + d) % 4 for d in range(4)]
     cs = [(gy % 2 + d) % 2 for d in range(2)]
-    zy = [[(z * 4 + v) * GY for v in ys] for z in zs]
+    zy = [[z * 4 + v for v in ys] for z in zs]
     xc = [[v * 2 + c for c in cs] for v in xs]
-    peers = [zy[o[0]][o[1]] + xc[o[2]][o[3]] for o in OFFSETS]
+    peers = [(zy[o[0]][o[1]], xc[o[2]][o[3]]) for o in OFFSETS]
     alike = [to for o, to in zip(OFFSETS, peers) if o[3] == 0]
-    partner = zy[0][0] + xc[0][1]
+    partner = (zy[0][0], xc[0][1])
     chip = gx * (GY // 2) + gy // 2
     barrier = pltpu.get_barrier_semaphore()
 
@@ -119,7 +120,7 @@
     for copy in small + tiles + [big]:
         copy.start()
     for to in peers:
-        pl.semaphore_signal(barrier, inc=1, device_id=to, device_id_type=FLAT)
+        pl.semaphore_signal(barrier, inc=1, device_id=to, device_id_type=MESH)
     for copy in small:
         copy.wait()
     cosp = jnp.cos(params[1])
@@ -200,15 +201,14 @@
         return recv.at[pl.ds((2 * me + q) * ROWS, ROWS)]
 
     def send(q, among):
-        arrived = sem.at[1] if q == 0 else groups.at[gx]
         for to in among:
             pltpu.make_async_remote_copy(
-                src_ref=slab(q, to),
+                src_ref=slab(q, to[0] * GY + to[1]),
                 dst_ref=landing(q),
                 send_sem=sem.at[2 * q],
-                recv_sem=arrived,
+                recv_sem=sem.at[2 * q + 1],
                 device_id=to,
-                device_id_type=FLAT,
+                device_id_type=MESH,
             ).start()
 
     shift(0)
@@ -218,7 +218,6 @@
     send(0, peers)
     acc = compute(1, acc)
     part[...] = jnp.sum(acc, axis=0, keepdims=True).reshape(1, 1, 128)
-    send(1, peers[:8])
     for to in alike:
         pltpu.make_async_remote_copy(
             src_ref=part,
@@ -226,9 +225,9 @@
             send_sem=sem.at[4],
             recv_sem=sem.at[5],
             device_id=to,
-            device_id_type=FLAT,
+            device_id_type=MESH,
         ).start()
-    send(1, peers[8:])
+    send(1, peers)
     own = [pltpu.make_async_copy(slab(q, me), landing(q), sem.at[6 + q]) for q in range(2)]
     own.append(pltpu.make_async_copy(part, sums.at[pl.ds(chip, 1)], sem.at[8]))
     for copy in own:
@@ -238,44 +237,57 @@
     most = recv.at[pl.ds(0, (DEV - 1) * ROWS)]
     few = sums.at[pl.ds(0, DEV // 2 - 1)]
     pltpu.make_async_copy(few, few, sem.at[5]).wait()
-    halves[0] = jnp.sum(sums[...], axis=0)
+    total[...] = jnp.sum(sums[...], axis=0, keepdims=True)
     for ref, s in ((most, 0), (most, 2), (few, 4), (most, 1)):
         pltpu.make_async_copy(ref, ref, sem.at[s]).wait()
     swap = pltpu.make_async_remote_copy(
-        src_ref=halves.at[0],
-        dst_ref=halves.at[1],
-        send_sem=sem.at[10],
-        recv_sem=sem.at[11],
+        src_ref=total,
+        dst_ref=totals.at[pl.ds(1, 1)],
+        send_sem=sem.at[9],
+        recv_sem=sem.at[10],
         device_id=partner,
-        device_id_type=FLAT,
+        device_id_type=MESH,
     )
     swap.start()
+    keep = pltpu.make_async_copy(total, totals.at[pl.ds(0, 1)], sem.at[11])
+    keep.start()
+    keep.wait()
     swap.wait()
-    level = jnp.sum(halves[...]) / COUNT + 1e-6
-    scale = 1.0 / jnp.full((8, 128), level, f32)
+    pltpu.make_async_copy(most, most, sem.at[3]).wait()
+
+
+def place_kernel(recv, totals, out, rows, both, placed, sem):
+    step_rows = DEV * ROWS * 2 // CHUNKS
+    step_lines = GX * TX // CHUNKS
+    first = pltpu.make_async_copy(totals, both, sem.at[CHUNKS])
+    first.start()
+    chunks = []
+    for i in range(CHUNKS):
+        at = pl.ds(i * step_rows, step_rows)
+        chunks.append(pltpu.make_async_copy(recv.at[at], rows.at[at], sem.at[i]))
+        chunks[-1].start()
+    first.wait()
+    level = jnp.sum(both[...]) / COUNT + 1e-6
+    scale = 1.0 / jnp.full((8, 128), level, jnp.float32)
     lane = lax.broadcasted_iota(jnp.int32, (8, 128), 1) // TY
-    line = lax.broadcasted_iota(jnp.int32, (8, 128), 0) // 2
-    step = (line - lane) % 4
-    around = sorted(itertools.product(range(4), repeat=2), key=lambda o: -hops(o + (0,)))
-    for batch in (around[:5], around[5:11], around[11:]):
-        sources = [zs[-dz % 4] * 4 + ys[-dy % 4] for dz, dy in batch]
-        for (dz, dy), source in zip(batch, sources):
-            block = recv.at[pl.ds(0, (GY if dz or dy else GY - 1) * ROWS)]
-            pltpu.make_async_copy(block, block, groups.at[source]).wait()
-        for source in sources:
-            x0 = pl.multiple_of(source * TX, TX)
+    pair = lax.broadcasted_iota(jnp.int32, (8, 128), 0) // 2
+    step = (pair - lane) % 4
+    for i in range(CHUNKS):
+        chunks[i].wait()
+        for source in range(i * GX // CHUNKS, (i + 1) * GX // CHUNKS):
             for h in range(2):
                 for r in range(ROWS):
-                    v = recv[pl.ds((source * GY + 4 * h) * 2 * ROWS + r, 8, stride=ROWS), :]
+                    v = rows[pl.ds((source * GY + 4 * h) * 2 * ROWS + r, 8, stride=ROWS), :]
                     w = v
                     for k in range(1, 4):
                         turned = pltpu.roll(pltpu.roll(v, 2 * k, 0), 128 - TY * k, 1)
                         w = jnp.where(step == k, turned, w)
-                    placed[r, pl.ds(x0, TX), h * 128 : (h + 1) * 128] = jnp.log(1.0 + w * scale)
-            pltpu.make_async_copy(
-                placed.at[:, pl.ds(x0, TX)], out.at[:, pl.ds(x0, TX)], sem.at[9]
-            ).start()
-    pltpu.make_async_copy(placed, out, sem.at[9]).wait()
+                    placed[r, source * TX : (source + 1) * TX, h * 128 : (h + 1) * 128] = jnp.log(
+                        1.0 + w * scale
+                    )
+        at = pl.ds(i * step_lines, step_lines)
+        pltpu.make_async_copy(placed.at[:, at], out.at[:, at], sem.at[CHUNKS + 1]).start()
+    pltpu.make_async_copy(placed, out, sem.at[CHUNKS + 1]).wait()
 
 
 def on_device(spectra, resample_index, resample_weight, disp_phase, surface_block):
@@ -283,11 +295,14 @@
     bf16 = jnp.bfloat16
     hbm = pl.BlockSpec(memory_space=pltpu.HBM)
     table = jnp.asarray(base_table(), bf16)
-    return pl.pallas_call(
+    recv, totals = pl.pallas_call(
         main_kernel,
-        out_shape=jax.ShapeDtypeStruct((ROWS, GX * TX, GY * TY), f32),
+        out_shape=(
+            jax.ShapeDtypeStruct((DEV * ROWS * 2, 128), f32),
+            jax.ShapeDtypeStruct((2, 1, 128), f32),
+        ),
         in_specs=[hbm] * 6,
-        out_specs=hbm,
+        out_specs=[hbm] * 2,
         scratch_shapes=[
             pltpu.VMEM((2, LINES, NK), bf16),
             pltpu.VMEM((3, RADIX, BLOCK), f32),
@@ -300,13 +315,10 @@
             pltpu.VMEM((RADIX, LINES // 2, 2 * BLOCK), bf16),
             pltpu.VMEM((2 * KEEP * BLOCK, 128), f32),
             pltpu.VMEM((1, 1, 128), f32),
-            pltpu.VMEM((2, 1, 128), f32),
-            pltpu.VMEM((DEV * ROWS * 2, 128), f32),
+            pltpu.VMEM((1, 1, 128), f32),
             pltpu.VMEM((DEV // 2, 1, 128), f32),
-            pltpu.VMEM((ROWS, GX * TX, GY * TY), f32),
             pltpu.SemaphoreType.DMA((13,)),
             pltpu.SemaphoreType.DMA((12,)),
-            pltpu.SemaphoreType.DMA((GX,)),
         ],
         compiler_params=pltpu.CompilerParams(
             collective_id=0, has_side_effects=True, vmem_limit_bytes=VMEM_BYTES
@@ -320,6 +332,20 @@
         surface_block,
         table,
     )
+    return pl.pallas_call(
+        place_kernel,
+        out_shape=jax.ShapeDtypeStruct((ROWS, GX * TX, GY * TY), f32),
+        in_specs=[hbm] * 2,
+        out_specs=hbm,
+        scratch_shapes=[
+            pltpu.VMEM((DEV * ROWS * 2, 128), f32),
+            pltpu.VMEM((2, 1, 128), f32),
+            pltpu.VMEM((ROWS, GX * TX, GY * TY), f32),
+            pltpu.SemaphoreType.DMA((CHUNKS + 2,)),
+        ],
+        compiler_params=pltpu.CompilerParams(vmem_limit_bytes=VMEM_BYTES),
+        name="place",
+    )(recv, totals)
 
 def solution(mesh):
     return jax.shard_map(

time: 26 us -> 25.3 us (0.973)
  local copies, waits for them, and re-layouts: 1.99 us -> 0 us
  Pallas kernels: 23.8 us -> 25.1 us
    unnamed x1 -> x0, local copies, waits for them, and re-layouts: 1.99 us -> none
    pallas_call x1 -> x2, Pallas kernels: 23.8 us -> 25.1 us  [the longest x1 22.3 us: on_device(): pl.pallas_call(main_kernel, out_shape=(jax.ShapeDtypeStruct((DEV * ROWS *...]
where the time goes in v10:
time: 25.3 us; the launch traced here: 25.1 us
  Pallas kernels  25.1 us (99%)
    pallas_call x1, Pallas kernels, on_device(): pl.pallas_call(main_kernel, out_shape=(jax.ShapeDtypeStruct((DEV * ROWS *...  22.3 us
    pallas_call x1, Pallas kernels, on_device(): pl.pallas_call(place_kernel, out_shape=jax.ShapeDtypeStruct((ROWS, GX * T...  2.75 us

profile of v10, /device:TPU:1, one launch (start us, length us, event | category | flops | bytes accessed | tf_op | source)
XLA Modules:
  0.0 25.1 jit_solution(2105249382623892103)
XLA Ops:
  0.0 22.3 %main.1 = (f32[1280,128]{1,0:T(8,128)}, f32[2,1,128]{2,1,0:T(1,128)}) custom-call(bf16[8,32,2048]{2,1,0:T(8,128)(2,1)} %spectra.1, s32[16,128]{1,0:T(8,128)} %bitcast.3, f32[16,128]{1,0:T(8,128)} %bitcast.4, f32[16,128]{1,0:T(8,128)} %bitcast.5, s32[8,32]{1,0:T(8,128)} %surface.1, bf16[16,128,256]{2,1,0:T(8,128)(2,1)} %constant.2.clone.table), custom_call_target="tpu_custom_call" | custom-call | tf_op jit(solution)/shard_map/main/pallas_call | solution.py:298
  22.4 2.7 %place.1 = f32[5,128,256]{2,1,0:T(8,128)} custom-call(f32[1280,128]{1,0:T(8,128)} %get-tuple-element.7.recv, f32[2,1,128]{2,1,0:T(1,128)} %get-tuple-element.8.totals), custom_call_target="tpu_custom_call" | custom-call | tf_op jit(solution)/shard_map/place/pallas_call | solution.py:335

commit v11 on v10

--- a/solution.py
+++ b/solution.py
@@ -23,7 +23,7 @@
 COUNT = 128 * 256 * KEEP * BLOCK
 MESH = pl.DeviceIdType.MESH
 VMEM_BYTES = 67043328
-CHUNKS = 8
+CHUNKS = 2
 
 
 def base_table():
@@ -213,9 +213,9 @@
 
     shift(0)
     acc = compute(0, jnp.zeros((8, 128), f32))
-    shift(1)
     pl.semaphore_wait(barrier, DEV - 1)
     send(0, peers)
+    shift(1)
     acc = compute(1, acc)
     part[...] = jnp.sum(acc, axis=0, keepdims=True).reshape(1, 1, 128)
     for to in alike:

time: 25.3 us -> 24.7 us (0.976)
  Pallas kernels: 25.1 us -> 24.5 us
    pallas_call x1, Pallas kernels: 2.75 us -> 2.4 us  [on_device(): pl.pallas_call(place_kernel, out_shape=jax.ShapeDtypeStruct((ROWS, GX * T...]
where the time goes in v11:
time: 24.7 us; the launch traced here: 24.5 us
  Pallas kernels  24.5 us (99%)
    pallas_call x1, Pallas kernels, on_device(): pl.pallas_call(main_kernel, out_shape=(jax.ShapeDtypeStruct((DEV * ROWS *...  22.1 us
    pallas_call x1, Pallas kernels, on_device(): pl.pallas_call(place_kernel, out_shape=jax.ShapeDtypeStruct((ROWS, GX * T...  2.4 us

profile of v11, /device:TPU:1, one launch (start us, length us, event | category | flops | bytes accessed | tf_op | source)
XLA Modules:
  0.0 24.5 jit_solution(5473794191066722998)
XLA Ops:
  0.0 22.1 %main.1 = (f32[1280,128]{1,0:T(8,128)}, f32[2,1,128]{2,1,0:T(1,128)}) custom-call(bf16[8,32,2048]{2,1,0:T(8,128)(2,1)} %spectra.1, s32[16,128]{1,0:T(8,128)} %bitcast.3, f32[16,128]{1,0:T(8,128)} %bitcast.4, f32[16,128]{1,0:T(8,128)} %bitcast.5, s32[8,32]{1,0:T(8,128)} %surface.1, bf16[16,128,256]{2,1,0:T(8,128)(2,1)} %constant.2.clone.table), custom_call_target="tpu_custom_call" | custom-call | tf_op jit(solution)/shard_map/main/pallas_call | solution.py:298
  22.1 2.4 %place.1 = f32[5,128,256]{2,1,0:T(8,128)} custom-call(f32[1280,128]{1,0:T(8,128)} %get-tuple-element.7.recv, f32[2,1,128]{2,1,0:T(1,128)} %get-tuple-element.8.totals), custom_call_target="tpu_custom_call" | custom-call | tf_op jit(solution)/shard_map/place/pallas_call | solution.py:335

commit v12 on v11

--- a/solution.py
+++ b/solution.py
@@ -77,10 +77,30 @@
     return sum((0, 1, 2, 1)[v] for v in o[:3])
 
 
-OFFSETS = sorted(
+FAR_FIRST = sorted(
     [o for o in itertools.product(range(4), range(4), range(4), range(2)) if any(o)],
     key=lambda o: (-hops(o), o),
 )
+
+
+def first_link(o):
+    for d in (2, 1, 0):
+        if o[d]:
+            return 3 * d + o[d]
+    return 0
+
+
+def woven(offsets):
+    lanes = {}
+    for o in offsets:
+        lanes.setdefault(first_link(o), []).append(o)
+    keyed = [
+        ((i + 0.5) / len(lane), link, o) for link, lane in lanes.items() for i, o in enumerate(lane)
+    ]
+    return [o for _, _, o in sorted(keyed)]
+
+
+OFFSETS = woven(FAR_FIRST)
 
 
 def main_kernel(
@@ -238,8 +258,8 @@
     few = sums.at[pl.ds(0, DEV // 2 - 1)]
     pltpu.make_async_copy(few, few, sem.at[5]).wait()
     total[...] = jnp.sum(sums[...], axis=0, keepdims=True)
-    for ref, s in ((most, 0), (most, 2), (few, 4), (most, 1)):
-        pltpu.make_async_copy(ref, ref, sem.at[s]).wait()
+    for s in (0, 1):
+        pltpu.make_async_copy(most, most, sem.at[s]).wait()
     swap = pltpu.make_async_remote_copy(
         src_ref=total,
         dst_ref=totals.at[pl.ds(1, 1)],
@@ -251,9 +271,10 @@
     swap.start()
     keep = pltpu.make_async_copy(total, totals.at[pl.ds(0, 1)], sem.at[11])
     keep.start()
+    for ref, s in ((most, 2), (few, 4), (most, 3)):
+        pltpu.make_async_copy(ref, ref, sem.at[s]).wait()
     keep.wait()
     swap.wait()
-    pltpu.make_async_copy(most, most, sem.at[3]).wait()
 
 
 def place_kernel(recv, totals, out, rows, both, placed, sem):

time: 24.7 us -> 24.7 us (level)
  no operation moved by 1% of the time
where the time goes in v12:
time: 24.7 us; the launch traced here: 24.6 us
  Pallas kernels  24.6 us (100%)
    pallas_call x1, Pallas kernels, on_device(): pl.pallas_call(main_kernel, out_shape=(jax.ShapeDtypeStruct((DEV * ROWS *...  22.2 us
    pallas_call x1, Pallas kernels, on_device(): pl.pallas_call(place_kernel, out_shape=jax.ShapeDtypeStruct((ROWS, GX * T...  2.4 us

profile of v12, /device:TPU:1, one launch (start us, length us, event | category | flops | bytes accessed | tf_op | source)
XLA Modules:
  0.0 24.6 jit_solution(7478140944774262392)
XLA Ops:
  0.0 22.2 %main.1 = (f32[1280,128]{1,0:T(8,128)}, f32[2,1,128]{2,1,0:T(1,128)}) custom-call(bf16[8,32,2048]{2,1,0:T(8,128)(2,1)} %spectra.1, s32[16,128]{1,0:T(8,128)} %bitcast.3, f32[16,128]{1,0:T(8,128)} %bitcast.4, f32[16,128]{1,0:T(8,128)} %bitcast.5, s32[8,32]{1,0:T(8,128)} %surface.1, bf16[16,128,256]{2,1,0:T(8,128)(2,1)} %constant.2.clone.table), custom_call_target="tpu_custom_call" | custom-call | tf_op jit(solution)/shard_map/main/pallas_call | solution.py:319
  22.2 2.4 %place.1 = f32[5,128,256]{2,1,0:T(8,128)} custom-call(f32[1280,128]{1,0:T(8,128)} %get-tuple-element.7.recv, f32[2,1,128]{2,1,0:T(1,128)} %get-tuple-element.8.totals), custom_call_target="tpu_custom_call" | custom-call | tf_op jit(solution)/shard_map/place/pallas_call | solution.py:356

commit v13 on v12

--- a/solution.py
+++ b/solution.py
@@ -24,6 +24,7 @@
 MESH = pl.DeviceIdType.MESH
 VMEM_BYTES = 67043328
 CHUNKS = 2
+LATE = 1
 
 
 def base_table():
@@ -117,7 +118,9 @@
     cs = [(gy % 2 + d) % 2 for d in range(2)]
     zy = [[z * 4 + v for v in ys] for z in zs]
     xc = [[v * 2 + c for c in cs] for v in xs]
-    peers = [(zy[o[0]][o[1]], xc[o[2]][o[3]]) for o in OFFSETS]
+    peers, greeted = (
+        [(zy[o[0]][o[1]], xc[o[2]][o[3]]) for o in order] for order in (OFFSETS, FAR_FIRST)
+    )
     alike = [to for o, to in zip(OFFSETS, peers) if o[3] == 0]
     partner = (zy[0][0], xc[0][1])
     chip = gx * (GY // 2) + gy // 2
@@ -139,7 +142,7 @@
     big = pltpu.make_async_copy(table, tab, load.at[12])
     for copy in small + tiles + [big]:
         copy.start()
-    for to in peers:
+    for to in greeted:
         pl.semaphore_signal(barrier, inc=1, device_id=to, device_id_type=MESH)
     for copy in small:
         copy.wait()
@@ -162,8 +165,10 @@
         lines = both[q, :half, :]
         both[q, half:, :] = jnp.concatenate([lines[:, 1:], lines[:, :1]], axis=1)
 
-    def compute(q, acc):
+    def compute(q, acc, meanwhile=None):
         for n in range(4):
+            if n == LATE and meanwhile is not None:
+                meanwhile()
             for e in range(2):
                 if q == 0:
                     pick = jnp.concatenate(
@@ -233,10 +238,12 @@
 
     shift(0)
     acc = compute(0, jnp.zeros((8, 128), f32))
-    pl.semaphore_wait(barrier, DEV - 1)
-    send(0, peers)
+    def release():
+        pl.semaphore_wait(barrier, DEV - 1)
+        send(0, peers)
+
     shift(1)
-    acc = compute(1, acc)
+    acc = compute(1, acc, release)
     part[...] = jnp.sum(acc, axis=0, keepdims=True).reshape(1, 1, 128)
     for to in alike:
         pltpu.make_async_remote_copy(

time: 24.7 us -> 24.9 us (level)
  no operation moved by 1% of the time
where the time goes in v13:
time: 24.9 us; the launch traced here: 24.8 us
  Pallas kernels  24.8 us (100%)
    pallas_call x1, Pallas kernels, on_device(): pl.pallas_call(main_kernel, out_shape=(jax.ShapeDtypeStruct((DEV * ROWS *...  22.4 us
    pallas_call x1, Pallas kernels, on_device(): pl.pallas_call(place_kernel, out_shape=jax.ShapeDtypeStruct((ROWS, GX * T...  2.4 us

profile of v13, /device:TPU:1, one launch (start us, length us, event | category | flops | bytes accessed | tf_op | source)
XLA Modules:
  0.0 24.8 jit_solution(13968478806925770846)
XLA Ops:
  0.0 22.4 %main.1 = (f32[1280,128]{1,0:T(8,128)}, f32[2,1,128]{2,1,0:T(1,128)}) custom-call(bf16[8,32,2048]{2,1,0:T(8,128)(2,1)} %spectra.1, s32[16,128]{1,0:T(8,128)} %bitcast.3, f32[16,128]{1,0:T(8,128)} %bitcast.4, f32[16,128]{1,0:T(8,128)} %bitcast.5, s32[8,32]{1,0:T(8,128)} %surface.1, bf16[16,128,256]{2,1,0:T(8,128)(2,1)} %constant.2.clone.table), custom_call_target="tpu_custom_call" | custom-call | tf_op jit(solution)/shard_map/main/pallas_call | solution.py:326
  22.4 2.4 %place.1 = f32[5,128,256]{2,1,0:T(8,128)} custom-call(f32[1280,128]{1,0:T(8,128)} %get-tuple-element.7.recv, f32[2,1,128]{2,1,0:T(1,128)} %get-tuple-element.8.totals), custom_call_target="tpu_custom_call" | custom-call | tf_op jit(solution)/shard_map/place/pallas_call | solution.py:363

commit v14 on v12

--- a/solution.py
+++ b/solution.py
@@ -117,7 +117,9 @@
     cs = [(gy % 2 + d) % 2 for d in range(2)]
     zy = [[z * 4 + v for v in ys] for z in zs]
     xc = [[v * 2 + c for c in cs] for v in xs]
-    peers = [(zy[o[0]][o[1]], xc[o[2]][o[3]]) for o in OFFSETS]
+    peers, greeted = (
+        [(zy[o[0]][o[1]], xc[o[2]][o[3]]) for o in order] for order in (OFFSETS, FAR_FIRST)
+    )
     alike = [to for o, to in zip(OFFSETS, peers) if o[3] == 0]
     partner = (zy[0][0], xc[0][1])
     chip = gx * (GY // 2) + gy // 2
@@ -139,7 +141,7 @@
     big = pltpu.make_async_copy(table, tab, load.at[12])
     for copy in small + tiles + [big]:
         copy.start()
-    for to in peers:
+    for to in greeted:
         pl.semaphore_signal(barrier, inc=1, device_id=to, device_id_type=MESH)
     for copy in small:
         copy.wait()
@@ -234,7 +236,7 @@
     shift(0)
     acc = compute(0, jnp.zeros((8, 128), f32))
     pl.semaphore_wait(barrier, DEV - 1)
-    send(0, peers)
+    send(0, peers[::-1])
     shift(1)
     acc = compute(1, acc)
     part[...] = jnp.sum(acc, axis=0, keepdims=True).reshape(1, 1, 128)

time: 24.7 us -> 25.4 us (1.028)
  Pallas kernels: 24.6 us -> 25.3 us
    pallas_call x1, Pallas kernels: 22.2 us -> 22.9 us  [on_device(): pl.pallas_call(main_kernel, out_shape=(jax.ShapeDtypeStruct((DEV * ROWS *...]
where the time goes in v14:
time: 25.4 us; the launch traced here: 25.3 us
  Pallas kernels  25.3 us (100%)
    pallas_call x1, Pallas kernels, on_device(): pl.pallas_call(main_kernel, out_shape=(jax.ShapeDtypeStruct((DEV * ROWS *...  22.9 us
    pallas_call x1, Pallas kernels, on_device(): pl.pallas_call(place_kernel, out_shape=jax.ShapeDtypeStruct((ROWS, GX * T...  2.4 us

profile of v14, /device:TPU:1, one launch (start us, length us, event | category | flops | bytes accessed | tf_op | source)
XLA Modules:
  0.0 25.3 jit_solution(15593913546475114072)
XLA Ops:
  0.0 22.9 %main.1 = (f32[1280,128]{1,0:T(8,128)}, f32[2,1,128]{2,1,0:T(1,128)}) custom-call(bf16[8,32,2048]{2,1,0:T(8,128)(2,1)} %spectra.1, s32[16,128]{1,0:T(8,128)} %bitcast.3, f32[16,128]{1,0:T(8,128)} %bitcast.4, f32[16,128]{1,0:T(8,128)} %bitcast.5, s32[8,32]{1,0:T(8,128)} %surface.1, bf16[16,128,256]{2,1,0:T(8,128)(2,1)} %constant.2.clone.table), custom_call_target="tpu_custom_call" | custom-call | tf_op jit(solution)/shard_map/main/pallas_call | solution.py:321
  22.9 2.4 %place.1 = f32[5,128,256]{2,1,0:T(8,128)} custom-call(f32[1280,128]{1,0:T(8,128)} %get-tuple-element.7.recv, f32[2,1,128]{2,1,0:T(1,128)} %get-tuple-element.8.totals), custom_call_target="tpu_custom_call" | custom-call | tf_op jit(solution)/shard_map/place/pallas_call | solution.py:358

commit v15 on v14

--- a/solution.py
+++ b/solution.py
@@ -236,7 +236,7 @@
     shift(0)
     acc = compute(0, jnp.zeros((8, 128), f32))
     pl.semaphore_wait(barrier, DEV - 1)
-    send(0, peers[::-1])
+    send(0, peers)
     shift(1)
     acc = compute(1, acc)
     part[...] = jnp.sum(acc, axis=0, keepdims=True).reshape(1, 1, 128)

time: 25.4 us -> 24.7 us (0.972)
  Pallas kernels: 25.3 us -> 24.6 us
    pallas_call x1, Pallas kernels: 22.9 us -> 22.2 us  [on_device(): pl.pallas_call(main_kernel, out_shape=(jax.ShapeDtypeStruct((DEV * ROWS *...]
where the time goes in v15:
time: 24.7 us; the launch traced here: 24.6 us
  Pallas kernels  24.6 us (100%)
    pallas_call x1, Pallas kernels, on_device(): pl.pallas_call(main_kernel, out_shape=(jax.ShapeDtypeStruct((DEV * ROWS *...  22.2 us
    pallas_call x1, Pallas kernels, on_device(): pl.pallas_call(place_kernel, out_shape=jax.ShapeDtypeStruct((ROWS, GX * T...  2.4 us

profile of v15, /device:TPU:1, one launch (start us, length us, event | category | flops | bytes accessed | tf_op | source)
XLA Modules:
  0.0 24.6 jit_solution(2064438985739558421)
XLA Ops:
  0.0 22.2 %main.1 = (f32[1280,128]{1,0:T(8,128)}, f32[2,1,128]{2,1,0:T(1,128)}) custom-call(bf16[8,32,2048]{2,1,0:T(8,128)(2,1)} %spectra.1, s32[16,128]{1,0:T(8,128)} %bitcast.3, f32[16,128]{1,0:T(8,128)} %bitcast.4, f32[16,128]{1,0:T(8,128)} %bitcast.5, s32[8,32]{1,0:T(8,128)} %surface.1, bf16[16,128,256]{2,1,0:T(8,128)(2,1)} %constant.2.clone.table), custom_call_target="tpu_custom_call" | custom-call | tf_op jit(solution)/shard_map/main/pallas_call | solution.py:321
  22.2 2.4 %place.1 = f32[5,128,256]{2,1,0:T(8,128)} custom-call(f32[1280,128]{1,0:T(8,128)} %get-tuple-element.7.recv, f32[2,1,128]{2,1,0:T(1,128)} %get-tuple-element.8.totals), custom_call_target="tpu_custom_call" | custom-call | tf_op jit(solution)/shard_map/place/pallas_call | solution.py:358

commit v16 on v11

--- a/solution.py
+++ b/solution.py
@@ -238,8 +238,8 @@
     few = sums.at[pl.ds(0, DEV // 2 - 1)]
     pltpu.make_async_copy(few, few, sem.at[5]).wait()
     total[...] = jnp.sum(sums[...], axis=0, keepdims=True)
-    for ref, s in ((most, 0), (most, 2), (few, 4), (most, 1)):
-        pltpu.make_async_copy(ref, ref, sem.at[s]).wait()
+    for s in (0, 1):
+        pltpu.make_async_copy(most, most, sem.at[s]).wait()
     swap = pltpu.make_async_remote_copy(
         src_ref=total,
         dst_ref=totals.at[pl.ds(1, 1)],
@@ -251,9 +251,10 @@
     swap.start()
     keep = pltpu.make_async_copy(total, totals.at[pl.ds(0, 1)], sem.at[11])
     keep.start()
+    for ref, s in ((most, 2), (few, 4), (most, 3)):
+        pltpu.make_async_copy(ref, ref, sem.at[s]).wait()
     keep.wait()
     swap.wait()
-    pltpu.make_async_copy(most, most, sem.at[3]).wait()
 
 
 def place_kernel(recv, totals, out, rows, both, placed, sem):

time: 24.7 us -> 24.7 us (level)
  no operation moved by 1% of the time
where the time goes in v16:
time: 24.7 us; the launch traced here: 24.5 us
  Pallas kernels  24.5 us (99%)
    pallas_call x1, Pallas kernels, on_device(): pl.pallas_call(main_kernel, out_shape=(jax.ShapeDtypeStruct((DEV * ROWS *...  22.1 us
    pallas_call x1, Pallas kernels, on_device(): pl.pallas_call(place_kernel, out_shape=jax.ShapeDtypeStruct((ROWS, GX * T...  2.4 us

profile of v16, /device:TPU:1, one launch (start us, length us, event | category | flops | bytes accessed | tf_op | source)
XLA Modules:
  0.0 24.5 jit_solution(9675477142377224990)
XLA Ops:
  0.0 22.1 %main.1 = (f32[1280,128]{1,0:T(8,128)}, f32[2,1,128]{2,1,0:T(1,128)}) custom-call(bf16[8,32,2048]{2,1,0:T(8,128)(2,1)} %spectra.1, s32[16,128]{1,0:T(8,128)} %bitcast.3, f32[16,128]{1,0:T(8,128)} %bitcast.4, f32[16,128]{1,0:T(8,128)} %bitcast.5, s32[8,32]{1,0:T(8,128)} %surface.1, bf16[16,128,256]{2,1,0:T(8,128)(2,1)} %constant.2.clone.table), custom_call_target="tpu_custom_call" | custom-call | tf_op jit(solution)/shard_map/main/pallas_call | solution.py:299
  22.1 2.4 %place.1 = f32[5,128,256]{2,1,0:T(8,128)} custom-call(f32[1280,128]{1,0:T(8,128)} %get-tuple-element.7.recv, f32[2,1,128]{2,1,0:T(1,128)} %get-tuple-element.8.totals), custom_call_target="tpu_custom_call" | custom-call | tf_op jit(solution)/shard_map/place/pallas_call | solution.py:336
